TPU v7x, 32 devices: a 4x4x1 block of a 4x4x8 slice. The times are simulated.
32 devices in a mesh: dp: 1 (over z), tp: 4 (over y), ep: 8 (over x, core).
Axes of the slice: x: 4, y: 4, z: 1, core: 2. Of those that a mesh axis runs over, the one named last changes fastest.
The devices are a block of a 4x4x8 slice.
Arguments:
- x_in: bfloat16 [4096, 1024], P(('dp', 'ep', 'tp'))
- norm_gain: bfloat16 [1024], replicated
- w_router: bfloat16 [1024, 32], replicated
- expert_idx: int32 [4096, 8], P(('dp', 'ep', 'tp'))
- w_gate: bfloat16 [32, 1024, 512], P('ep', None, 'tp')
- w_up: bfloat16 [32, 1024, 512], P('ep', None, 'tp')
- w_down: bfloat16 [32, 512, 1024], P('ep', 'tp')
- out_bias: bfloat16 [1024], replicated
- dy_out: bfloat16 [4096, 1024], P(('dp', 'ep', 'tp'))
Outputs:
- output 1: bfloat16 [4096, 1024], P(('dp', 'ep', 'tp'))
- output 2: bfloat16 [4096, 1024], P(('dp', 'ep', 'tp'))
- output 3: float32 [1024], P('dp')
- output 4: float32 [1024, 32], P('dp')
- output 5: float32 [32, 1024, 512], P(('dp', 'ep'), None, 'tp')
- output 6: float32 [32, 1024, 512], P(('dp', 'ep'), None, 'tp')
- output 7: float32 [32, 512, 1024], P(('dp', 'ep'), 'tp')
- output 8: float32 [1024], P('dp')
All inputs are finite; a program needn't handle non-finite values.
Results may differ from a plain program's by a relative error of at most 0.0135311.
Values are sent between devices in bfloat16 or wider.
A program may use at most 768 MiB of HBM per device.

v0:
```python
import jax
import jax.numpy as jnp
from jax import lax
from jax.sharding import PartitionSpec as P

EPS = 1e-6


def routing_tables(expert_ids, n_exp, capacity):
    n_tok, top_k = expert_ids.shape
    flat_ids = expert_ids.reshape(-1)
    order = jnp.argsort(flat_ids, stable=True)
    counts = jnp.sum((flat_ids[:, None] == jnp.arange(n_exp)[None, :]).astype(jnp.int32), axis=0)
    starts = jnp.cumsum(counts) - counts
    slot_rank = jnp.arange(capacity)[None, :]
    slot_copy = order[jnp.minimum(starts[:, None] + slot_rank, n_tok * top_k - 1)]
    slot_ok = slot_rank < counts[:, None]
    copy_pos = flat_ids * capacity + jnp.argsort(order) - starts[flat_ids]
    return slot_copy, slot_ok, copy_pos.reshape(n_tok, top_k)


def solution(mesh):
    tok_spec = P(("dp", "ep", "tp"), None)
    wide_spec = P("ep", None, "tp")
    down_spec = P("ep", "tp", None)
    grad_wide = P(("dp", "ep"), None, "tp")
    grad_down = P(("dp", "ep"), "tp", None)

    def device_step(x_in, norm_gain, w_router, expert_idx, w_gate, w_up, w_down, out_bias, dy_out):
        n_tok, d_model = x_in.shape
        n_exp = w_router.shape[1]
        top_k = expert_idx.shape[1]
        local_exp = w_gate.shape[0]
        n_ep = n_exp // local_exp
        capacity = (2 * n_tok * top_k + n_exp - 1) // n_exp
        x_f32 = x_in.astype(jnp.float32)
        inv_rms = lax.rsqrt(jnp.mean(x_f32 * x_f32, axis=-1, keepdims=True) + EPS)
        normed = x_f32 * inv_rms
        gain_f32 = norm_gain.astype(jnp.float32)
        hidden = (normed * gain_f32).astype(jnp.bfloat16)
        logits = jnp.dot(hidden, w_router, preferred_element_type=jnp.float32)
        chosen = expert_idx[:, :, None] == jnp.arange(n_exp)[None, None, :]
        gates = jax.nn.softmax(jnp.sum(jnp.where(chosen, logits[:, None, :], 0.0), axis=-1), axis=-1)
        slot_copy, slot_ok, copy_pos = routing_tables(expert_idx, n_exp, capacity)
        place_shape = (n_ep, local_exp, capacity, d_model)
        send_rows = jnp.where(slot_ok[:, :, None], hidden[slot_copy // top_k], 0).reshape(place_shape)
        recv_rows = lax.all_to_all(send_rows, "ep", 0, 0, tiled=True)
        rows_in = lax.all_gather(recv_rows, "tp", axis=0)
        gate_pre = jnp.einsum("tsmcd,mdf->tsmcf", rows_in, w_gate, preferred_element_type=jnp.float32)
        up_pre = jnp.einsum("tsmcd,mdf->tsmcf", rows_in, w_up, preferred_element_type=jnp.float32)
        sigma_gate = jax.nn.sigmoid(gate_pre)
        silu_gate = gate_pre * sigma_gate
        hidden_act = (silu_gate * up_pre).astype(jnp.bfloat16)
        part_out = jnp.einsum("tsmcf,mfd->tsmcd", hidden_act, w_down, preferred_element_type=jnp.float32).astype(jnp.bfloat16)
        y_recv = lax.psum_scatter(part_out, "tp", scatter_dimension=0, tiled=True)[0]
        y_slots = lax.all_to_all(y_recv, "ep", 0, 0, tiled=True).reshape(n_exp * capacity, d_model)
        y_copy = y_slots[copy_pos].astype(jnp.float32)
        moe_out = jnp.sum(gates[:, :, None] * y_copy, axis=1) + out_bias.astype(jnp.float32)
        y_out = (x_f32 + moe_out).astype(jnp.bfloat16)
        dy_f32 = dy_out.astype(jnp.float32)
        d_bias = jnp.sum(dy_f32, axis=0)
        d_gates = jnp.sum(dy_f32[:, None, :] * y_copy, axis=-1)
        dy_copy = (gates[:, :, None] * dy_f32[:, None, :]).astype(jnp.bfloat16).reshape(n_tok * top_k, d_model)
        d_send = jnp.where(slot_ok[:, :, None], dy_copy[slot_copy], 0).reshape(place_shape)
        d_recv = lax.all_to_all(d_send, "ep", 0, 0, tiled=True)
        d_rows = lax.all_gather(d_recv, "tp", axis=0)
        d_act = jnp.einsum("tsmcd,mfd->tsmcf", d_rows, w_down, preferred_element_type=jnp.float32)
        d_down = jnp.einsum("tsmcf,tsmcd->mfd", hidden_act, d_rows, preferred_element_type=jnp.float32)
        d_gate_pre = (d_act * up_pre * sigma_gate * (1.0 + gate_pre * (1.0 - sigma_gate))).astype(jnp.bfloat16)
        d_up_pre = (d_act * silu_gate).astype(jnp.bfloat16)
        d_gate = jnp.einsum("tsmcd,tsmcf->mdf", rows_in, d_gate_pre, preferred_element_type=jnp.float32)
        d_up = jnp.einsum("tsmcd,tsmcf->mdf", rows_in, d_up_pre, preferred_element_type=jnp.float32)
        dh_part = (jnp.einsum("tsmcf,mdf->tsmcd", d_gate_pre, w_gate, preferred_element_type=jnp.float32) + jnp.einsum("tsmcf,mdf->tsmcd", d_up_pre, w_up, preferred_element_type=jnp.float32)).astype(jnp.bfloat16)
        dh_recv = lax.psum_scatter(dh_part, "tp", scatter_dimension=0, tiled=True)[0]
        dh_slots = lax.all_to_all(dh_recv, "ep", 0, 0, tiled=True).reshape(n_exp * capacity, d_model)
        dh_expert = jnp.sum(dh_slots[copy_pos].astype(jnp.float32), axis=1)
        d_chosen = gates * (d_gates - jnp.sum(gates * d_gates, axis=-1, keepdims=True))
        d_logits = jnp.sum(jnp.where(chosen, d_chosen[:, :, None], 0.0), axis=1)
        d_router = jnp.einsum("td,te->de", hidden, d_logits, preferred_element_type=jnp.float32)
        dh_total = dh_expert + jnp.einsum("te,de->td", d_logits, w_router, preferred_element_type=jnp.float32)
        d_gain = jnp.sum(dh_total * normed, axis=0)
        d_norm = dh_total * gain_f32
        dx_in = (dy_f32 + inv_rms * (d_norm - normed * jnp.mean(d_norm * normed, axis=-1, keepdims=True))).astype(jnp.bfloat16)
        d_gain, d_router, d_bias = lax.psum((d_gain, d_router, d_bias), ("ep", "tp"))
        return y_out, dx_in, d_gain, d_router, d_gate, d_up, d_down, d_bias

    return jax.shard_map(device_step, mesh=mesh, in_specs=(tok_spec, P(None), P(None, None), tok_spec, wide_spec, wide_spec, down_spec, P(None), tok_spec), out_specs=(tok_spec, tok_spec, P("dp"), P("dp", None), grad_wide, grad_wide, grad_down, P("dp")), check_vma=False)
```

profile of v0, /device:TPU:97, one launch (start us, length us, event | category | flops | bytes accessed | tf_op | source)
XLA Modules:
  0.0 1258.6 jit_solution(11550918415644682206)
XLA Ops:
  7.3 1.2 fusion.58
  8.4 0.7 convert_element_type.59
  9.1 0.8 copy.91
  10.3 4.4 sort.34
  15.1 8.6 gather_fusion
  25.2 0.9 convert_element_type.68
  26.1 9.7 gather_fusion.1
  35.7 1.3 fusion.13
  37.1 9.7 gather_fusion.3
  46.8 5.2 broadcast_select_fusion
  51.9 54.4 %all_to_all.20 = bf16[8,4,64,1024]{3,2,1,0:T(8,128)(2,1)} all-to-all(bf16[8,4,64,1024]{3,2,1,0:T(8,128)(2,1)S(1)} %get-tuple-element.56), channel_id=1, replica_groups=mesh['dp'=1,'tp'=4,'ep'=8] {'ep'}, dimensions={0} | all-to-all | bytes 8388608 | tf_op jit(solution)/shard_map/all_to_all | solution.py:47
  106.5 54.0 %all_to_all.21 = bf16[8,4,64,1024]{3,2,1,0:T(8,128)(2,1)} all-to-all(bf16[8,4,64,1024]{3,2,1,0:T(8,128)(2,1)} %get-tuple-element.55), channel_id=1, replica_groups=mesh['dp'=1,'tp'=4,'ep'=8] {'ep'}, dimensions={0} | all-to-all | bytes 8388608 | tf_op jit(solution)/shard_map/all_to_all | solution.py:65
  160.8 99.3 %all-gather.5.cloned.1.call-done = bf16[32,4,64,1024]{3,2,1,0:T(8,128)(2,1)} async-done(((bf16[8,4,64,1024]{3,2,1,0:T(8,128)(2,1)}), bf16[32,4,64,1024]{3,2,1,0:T(8,128)(2,1)}) %all-gather.5.cloned.1.call-update) | async-done | bytes 16777232 | tf_op jit(solution)/shard_map/all_gather | solution.py:48
  260.2 14.1 %copy.93 = bf16[32,4,64,1024]{3,2,0,1:T(8,128)(2,1)} copy(bf16[32,4,64,1024]{3,2,1,0:T(8,128)(2,1)} %all-gather.5.cloned.1.call-done) | data formatting | bytes 33554432 | tf_op jit(solution)/shard_map/all_gather | solution.py:48
  274.3 10.2 fusion.38
  284.5 10.1 fusion.42
  294.6 120.5 %all-gather.7.cloned.1.call-done = bf16[32,4,64,1024]{3,2,1,0:T(8,128)(2,1)} async-done(((bf16[8,4,64,1024]{3,2,1,0:T(8,128)(2,1)}), bf16[32,4,64,1024]{3,2,1,0:T(8,128)(2,1)}) %all-gather.7.cloned.1.call-update) | async-done | bytes 16777232 | tf_op jit(solution)/shard_map/all_gather | solution.py:66
  415.1 14.1 %copy.97 = bf16[32,4,64,1024]{3,2,0,1:T(8,128)(2,1)} copy(bf16[32,4,64,1024]{3,2,1,0:T(8,128)(2,1)} %all-gather.7.cloned.1.call-done) | data formatting | bytes 33554432 | tf_op jit(solution)/shard_map/all_gather | solution.py:66
  429.2 17.0 %fusion.12 = (bf16[4,8,4,64,128]{4,3,1,0,2:T(8,128)(2,1)}, bf16[4,8,4,64,128]{4,3,1,0,2:T(8,128)(2,1)}, bf16[4,8,4,64,128]{4,3,1,0,2:T(8,128)(2,1)}) fusion(f32[4,4,8,64,128]{4,3,2,1,0:T(8,128)} %fusion.42, f32[4,4,8,64,128]{4,3,2,1,0:T(8,128)} %fusion.38, bf16[4,8,4,64,1024]{4,3,1,0,2:T(8,128)(2,1)} %bitcast.179, bf16[4,128,1024]{2,1,0:T(8,128)(2,1)S(1)} %copy-done), kind=kOutput, calls=%fused_computation.26 | convolution fusion | flops 2163212288 | bytes 32505856 | tf_op jit(solution)/shard_map/tsmcd,mfd->tsmcf/dot_general | solution.py:67
  446.2 10.0 convert_bitcast_fusion
  456.2 14.9 %fusion.40 = f32[4,4,8,64,1024]{4,3,2,1,0:T(8,128)} fusion(bf16[4,8,4,64,128]{4,3,1,0,2:T(8,128)(2,1)} %get-tuple-element.48, bf16[4,1024,128]{2,1,0:T(8,128)(2,1)S(1)} %copy-done.7), kind=kOutput, calls=%fused_computation.50 | convolution fusion | flops 2147483648 | bytes 36700160 | tf_op jit(solution)/shard_map/tsmcf,mdf->tsmcd/dot_general | solution.py:73
  471.1 16.8 %fusion = bf16[4,8,4,64,1024]{4,3,1,0,2:T(8,128)(2,1)} fusion(f32[4,4,8,64,1024]{4,3,2,1,0:T(8,128)} %fusion.40, bf16[4,8,4,64,128]{4,3,1,0,2:T(8,128)(2,1)S(1)} %copy-done.10, bf16[4,1024,128]{2,1,0:T(8,128)(2,1)S(1)} %copy-done.8), kind=kOutput, calls=%fused_computation.6 | convolution fusion | flops 2164260864 | bytes 53477376 | tf_op jit(solution)/shard_map/tsmcf,mdf->tsmcd/dot_general | solution.py:73
  489.2 559.9 %all-reduce.9.cloned.1.call-done = (bf16[4,8,4,64,1024]{4,3,1,0,2:T(8,128)(2,1)}, bf16[4,8,4,64,1024]{4,3,1,0,2:T(8,128)(2,1)}) async-done(((bf16[4,8,4,64,1024]{4,3,1,0,2:T(8,128)(2,1)}, bf16[4,8,4,64,1024]{4,3,1,0,2:T(8,128)(2,1)}), (bf16[4,8,4,64,1024]{4,3,1,0,2:T(8,128)(2,1)}, bf16[4,8,4,64,1024]{4,3,1,0,2:T(8,128)(2,1)})) %all-reduce.9.cloned.1.call-update) | async-done | bytes 33554448
  1049.0 3.3 dynamic-slice_bitcast_fusion.1
  1052.3 2.4 copy.94
  1054.8 5.5 all-to-all-start.1
  1060.4 4.4 sort.35
  1064.7 0.7 fusion.65
  1065.4 0.7 fusion.64
  1066.2 4.4 compare_select_fusion.4
  1070.8 15.4 %select_subtract_fusion = s32[1024]{0:T(1024)S(1)} fusion(pred[1024]{0:T(1024)(128)(4,1)S(1)} %get-tuple-element.40, pred[1024]{0:T(1024)(128)(4,1)S(1)} %get-tuple-element.39, pred[1024]{0:T(1024)(128)(4,1)S(1)} %get-tuple-element.38, pred[1024]{0:T(1024)(128)(4,1)S(1)} %get-tuple-element.37, pred[1024]{0:T(1024)(128)(4,1)S(1)} %get-tuple-element.36, ...), kind=kLoop, calls=%fused_computation.126 | loop fusion | flops 28672 | bytes 42084 | tf_op jit(solution)/shard_map/sub | solution.py:18
  1086.5 3.3 dynamic-slice_bitcast_fusion
  1089.8 2.4 copy.98
  1092.2 16.7 %all-to-all-done.1 = bf16[8,4,64,1024]{3,2,1,0:T(8,128)(2,1)} async-done(((bf16[8,4,64,1024]{3,2,1,0:T(8,128)(2,1)}), bf16[8,4,64,1024]{3,2,1,0:T(8,128)(2,1)}, u32[]{:S(2)}, u32[]{:S(2)}) %all-to-all-start.1) | async-done | bytes 4194336 | tf_op jit(solution)/shard_map/all_to_all | solution.py:56
  1108.9 5.5 all-to-all-start.3
  1114.4 9.7 fusion.32
  1124.2 11.7 fusion.27
  1135.9 11.1 fusion.22
  1147.0 7.8 gather_fusion.2
  1154.8 2.4 fusion.8
  1157.3 0.8 fusion.67
  1158.2 4.9 all-to-all-done.3
  1163.1 8.0 gather_fusion.4
  1171.1 1.4 convert_reduce_fusion
  1173.0 1.1 convert_reduce_fusion.1
  1174.1 44.1 %all-reduce.2 = (f32[1024]{0:T(1024)}, f32[1024]{0:T(1024)}) all-reduce(f32[1024]{0:T(1024)S(1)} %get-tuple-element.14, f32[1024]{0:T(1024)S(1)} %get-tuple-element.50), channel_id=1, replica_groups=mesh['dp'=1,'tp'=4,'ep'=8] {'ep','tp'}, use_global_device_ids=true, to_apply=%region_17.18 | all-reduce | flops 2048 | bytes 16384 | tf_op jit(solution)/shard_map/psum | solution.py:84
  1218.3 32.0 %all-reduce.7.cloned.1.call-done = f32[1024,32]{0,1:T(8,128)} async-done(((f32[1024,32]{0,1:T(8,128)}), f32[1024,32]{0,1:T(8,128)}) %all-reduce.7.cloned.1.call-update) | async-done | bytes 131088 | tf_op jit(solution)/shard_map/psum | solution.py:84
  1250.3 1.6 copy.147
  (118 shorter events, 5.3 us)
Async XLA Ops:
  7.2 422.0 %copy-start = (bf16[4,128,1024]{2,1,0:T(8,128)(2,1)S(1)}, bf16[4,128,1024]{2,1,0:T(8,128)(2,1)}, u32[]{:S(2)}) copy-start(bf16[4,128,1024]{2,1,0:T(8,128)(2,1)} %param.15) | copy-start | bytes 3145732
  7.2 253.0 %all-gather.5.cloned.1.call-start = ((), (), s32[]{:S(2)}) async-start(), calls=%async_computation.5 | async-start | bytes 20971520 | tf_op jit(solution)/shard_map/all_gather | solution.py:48
  8.4 15.6 %copy-start.30 = (f32[128]{0:T(128)}, f32[128]{0:T(128)S(1)}, u32[]{:S(2)}) copy-start(f32[128]{0:T(128)S(1)} %add_rsqrt_fusion) | copy-start | bytes 1540
  9.1 14.9 %copy-start.22 = (f32[1024]{0:T(1024)}, f32[1024]{0:T(1024)S(1)}, u32[]{:S(2)}) copy-start(f32[1024]{0:T(1024)S(1)} %convert_element_type.59) | copy-start | bytes 12292
  15.1 8.9 copy-start.5
  15.1 9.0 copy-start.18
  15.1 9.2 copy-start.24
  15.1 10.1 copy-start.14
  24.1 11.6 copy-start.2
  24.4 0.6 copy-start.20
  24.4 1.6 copy-start.26
  25.0 1.1 copy-start.28
  25.1 1.0 copy-start.16
  106.4 308.7 %all-gather.7.cloned.1.call-start = ((), (), s32[]{:S(2)}) async-start(), calls=%async_computation.6 | async-start | bytes 20971520 | tf_op jit(solution)/shard_map/all_gather | solution.py:66
  160.6 113.7 %copy-start.8 = (bf16[4,1024,128]{2,1,0:T(8,128)(2,1)S(1)}, bf16[4,1024,128]{2,1,0:T(8,128)(2,1)}, u32[]{:S(2)}) copy-start(bf16[4,1024,128]{2,1,0:T(8,128)(2,1)} %param.14) | copy-start | bytes 3145732
  160.6 888.4 %all-reduce.9.cloned.1.call-start = ((), (), s32[]{:S(2)}) async-start(), calls=%async_computation.7 | async-start | bytes 67108864
  274.3 10.2 copy-start.7
  456.2 14.9 %copy-start.10 = (bf16[4,8,4,64,128]{4,3,1,0,2:T(8,128)(2,1)S(1)}, bf16[4,8,4,64,128]{4,3,1,0,2:T(8,128)(2,1)}, u32[]{:S(2)}) copy-start(bf16[4,8,4,64,128]{4,3,1,0,2:T(8,128)(2,1)} %get-tuple-element.47) | copy-start | bytes 6291460
  487.9 0.7 copy-start.33
  1054.7 5.6 copy-start.32
  1054.8 54.2 %all-to-all-start.1 = ((bf16[8,4,64,1024]{3,2,1,0:T(8,128)(2,1)}), bf16[8,4,64,1024]{3,2,1,0:T(8,128)(2,1)}, u32[]{:S(2)}, u32[]{:S(2)}) async-start(bf16[8,4,64,1024]{3,2,1,0:T(8,128)(2,1)} %copy.94), calls=%async_computation.1 | async-start | bytes 8388608 | tf_op jit(solution)/shard_map/all_to_all | solution.py:56
  1092.2 22.2 %copy-start.12 = (bf16[4,8,4,64,128]{4,3,1,0,2:T(8,128)(2,1)S(1)}, bf16[4,8,4,64,128]{4,3,1,0,2:T(8,128)(2,1)}, u32[]{:S(2)}) copy-start(bf16[4,8,4,64,128]{4,3,1,0,2:T(8,128)(2,1)} %get-tuple-element.49) | copy-start | bytes 6291460
  1108.9 54.2 %all-to-all-start.3 = ((bf16[8,4,64,1024]{3,2,1,0:T(8,128)(2,1)}), bf16[8,4,64,1024]{3,2,1,0:T(8,128)(2,1)}, u32[]{:S(2)}, u32[]{:S(2)}) async-start(bf16[8,4,64,1024]{3,2,1,0:T(8,128)(2,1)} %copy.98), calls=%async_computation.3 | async-start | bytes 8388608 | tf_op jit(solution)/shard_map/all_to_all | solution.py:75
  1114.4 135.9 %all-reduce.7.cloned.1.call-start = ((), (), s32[]{:S(2)}) async-start(), calls=%async_computation.4 | async-start | bytes 262144 | tf_op jit(solution)/shard_map/psum | solution.py:84
  1114.4 9.8 copy-start.11
  1124.2 11.7 copy-start.9
  1147.0 7.8 copy-start.4
  1147.0 7.8 copy-start.17
  1147.0 10.2 copy-start.21
  1147.0 10.2 copy-start.27
  1147.0 10.2 copy-start.29
  1147.0 10.3 copy-start.25
  1147.0 10.3 copy-start.3
  1163.1 9.4 copy-start.6
  1163.1 9.5 copy-start.19
  1163.1 9.5 copy-start.23
  1163.1 9.5 copy-start.31
  1163.1 88.8 %copy-start.1 = (bf16[4,128,1024]{2,1,0:T(8,128)(2,1)S(1)}, bf16[4,128,1024]{2,1,0:T(8,128)(2,1)}, u32[]{:S(2)}) copy-start(bf16[4,128,1024]{2,1,0:T(8,128)(2,1)} %param.15) | copy-start | bytes 3145732
  1171.1 1.9 copy-start.13
  1171.1 1.9 copy-start.15
Sparse Core Ops, SparseCore 0:
  106.5 153.5 all-gather.4
  261.7 153.2 all-gather.6
  488.0 560.9 all-reduce.8
  1158.3 91.9 all-reduce.6
where the time goes:
time: 1260 us
  waiting for transfers between devices  834 us (66%)
  blocking collectives  153 us (12%)
  matrix products  113 us (9%)
  local copies, waits for them, and re-layouts  90.1 us (7%)
  other arithmetic  43.7 us (3%)
  between operations  14.4 us (1%)
    unnamed x5, waiting for transfers between devices  560 us
    all_gather x1, waiting for transfers between devices, device_step(): d_rows = lax.all_gather(d_recv, 'tp', axis=0)  121 us
    all_gather x1, waiting for transfers between devices, device_step(): rows_in = lax.all_gather(recv_rows, 'tp', axis=0)  99.3 us
    all_to_all x1, blocking collectives, device_step(): recv_rows = lax.all_to_all(send_rows, 'ep', 0, 0, tiled=True)  54.4 us
    all_to_all x1, blocking collectives, device_step(): d_recv = lax.all_to_all(d_send, 'ep', 0, 0, tiled=True)  54 us
    psum x1, blocking collectives, device_step(): lax.psum((d_gain, d_router, d_bias), ('ep', 'tp'))  44.1 us
    psum x1, waiting for transfers between devices, device_step(): lax.psum((d_gain, d_router, d_bias), ('ep', 'tp'))  32 us
  transfers between devices with their start and end apart: 6, of which 6 were waited for; matrix products, arithmetic and copies ran while one was open for 10% of the time, Pallas kernels for 0%

commit v1 on v0

v1 whole, which is shorter than its diff:
```python
import jax
import jax.numpy as jnp
from jax import lax
from jax.experimental import pallas as pl
from jax.experimental.pallas import tpu as pltpu
from jax.sharding import PartitionSpec as P

EPS = 1e-6
MESH = pl.DeviceIdType.MESH
F32 = jnp.float32
BF16 = jnp.bfloat16
ORDER = ((0, 0), (1, 0), (3, 0), (0, 1), (0, 3), (2, 0), (0, 2), (1, 1), (1, 3), (1, 2), (3, 1), (3, 3), (3, 2), (2, 1), (2, 3), (2, 2))
SLOT = {place: k for k, place in enumerate(ORDER)}
N_SLOT = len(ORDER)
N_SEND = 67
LAG = 2


def dot_nt(a, b):
    return lax.dot_general(a, b, (((1,), (1,)), ((), ())), preferred_element_type=F32)


def moe_kernel(h_ref, dy_ref, gate_ref, wg_ref, wu_ref, wd_ref,
               ysum_ref, dhsum_ref, dgate_ref, dbias_ref, dwg_ref, dwu_ref, dwd_ref,
               x_own, x_sib, part, g_own, g_sib, pg_own, pg_sib, q_buf, qg_buf,
               r1, r1g, r2, r2g, r3, r3g, r4, r4g, wgu, wd, acc_gu, acc_d, acc_b,
               load_sem, ag_send, ag_recv, ag_grecv, sib_recv,
               rq_send, rq_recv, s1_send, s1_recv, s2_send, s2_recv, f1_send, f1_recv, f2_send, f2_recv):
    ep = lax.axis_index("ep")
    tp = lax.axis_index("tp")
    n_tp = lax.axis_size("tp")
    n_x = lax.axis_size("ep") // 2
    core = lax.rem(ep, 2)
    chip_x = lax.div(ep, 2)
    n_loc, d_model, width = wg_ref.shape
    n_tok = h_ref.shape[0]
    n_exp = gate_ref.shape[0]
    loc = n_loc * width

    def shifted(x_step, y_step):
        x_new = lax.rem(chip_x + x_step + n_x, n_x)
        y_new = lax.rem(tp + y_step + n_tp, n_tp)
        return {"tp": y_new, "ep": 2 * x_new + core}

    f_up = shifted(1 - core, core)
    f_dn = shifted(core - 1, -core)
    s_up = shifted(core, 1 - core)
    s_dn = shifted(-core, core - 1)
    sib = {"ep": ep + 1 - 2 * core}

    loads = []
    for e in range(n_loc):
        cols = pl.ds(e * width, width)
        loads.append(pltpu.make_async_copy(wg_ref.at[e], wgu.at[:, cols], load_sem.at[len(loads)]))
        loads.append(pltpu.make_async_copy(wu_ref.at[e], wgu.at[:, pl.ds(loc + e * width, width)], load_sem.at[len(loads)]))
        loads.append(pltpu.make_async_copy(wd_ref.at[e], wd.at[cols], load_sem.at[len(loads)]))
    for c in loads:
        c.start()
    x_own[0, 0] = h_ref[...]
    x_own[0, 1] = dy_ref[...]
    g_own[0] = gate_ref[...]

    barrier = pltpu.get_barrier_semaphore()
    for dev in (f_up, f_dn, s_up, s_dn, sib):
        pl.semaphore_signal(barrier, inc=1, device_id=dev, device_id_type=MESH)
    pl.semaphore_wait(barrier, 5)

    def remote(src, dst, send, recv, dev):
        return pltpu.make_async_remote_copy(src_ref=src, dst_ref=dst, send_sem=send, recv_sem=recv, device_id=dev, device_id_type=MESH)

    sends = {k: [] for k in range(N_SLOT)}
    count = [0]

    def plan(k, src, dst, recv, dev):
        n = count[0]
        count[0] += 1
        sends[k].append(lambda: remote(src, dst, ag_send.at[n], recv, dev))

    def plan_block(k, to, dev):
        plan(k, x_own.at[k], x_own.at[to], ag_recv.at[to, 0], dev)
        plan(k, g_own.at[k], g_own.at[to], ag_grecv.at[to], dev)

    plan_block(0, SLOT[(3, 0)], f_up)
    plan_block(0, SLOT[(1, 0)], f_dn)
    for k, (df, ds) in enumerate(ORDER):
        if (df, ds) == (3, 0):
            to = SLOT[(2, 0)]
            plan(k, x_own.at[k, 0], x_own.at[to, 0], ag_recv.at[to, 0], f_up)
            plan(k, g_own.at[k], g_own.at[to], ag_grecv.at[to], f_up)
        if (df, ds) == (1, 0):
            to = SLOT[(2, 0)]
            plan(k, x_own.at[k, 1], x_own.at[to, 1], ag_recv.at[to, 1], f_dn)
        if ds == 0:
            plan_block(k, SLOT[(df, 3)], s_up)
            plan_block(k, SLOT[(df, 1)], s_dn)
        if ds == 3:
            to = SLOT[(df, 2)]
            plan(k, x_own.at[k, 0], x_own.at[to, 0], ag_recv.at[to, 0], s_up)
            plan(k, g_own.at[k], g_own.at[to], ag_grecv.at[to], s_up)
        if ds == 1:
            to = SLOT[(df, 2)]
            plan(k, x_own.at[k, 1], x_own.at[to, 1], ag_recv.at[to, 1], s_dn)
        plan(k, x_own.at[k], x_sib.at[k], sib_recv.at[k, 0], sib)
        plan(k, g_own.at[k], g_sib.at[k], sib_recv.at[k, 1], sib)
    assert count[0] == N_SEND

    def arrive(k):
        if k:
            if ORDER[k][1] == 2 or ORDER[k] == (2, 0):
                for t in range(2):
                    remote(x_own.at[k, t], x_own.at[k, t], ag_send.at[0], ag_recv.at[k, t], sib).wait_recv()
            else:
                remote(x_own.at[k], x_own.at[k], ag_send.at[0], ag_recv.at[k, 0], sib).wait_recv()
            remote(g_own.at[k], g_own.at[k], ag_send.at[0], ag_grecv.at[k], sib).wait_recv()
        for make in sends[k]:
            make().start()

    def to_sibling(k):
        return (remote(x_sib.at[k], q_buf.at[k], rq_send.at[k, 0], rq_recv.at[k, 0], sib),
                remote(pg_sib.at[k], qg_buf.at[k], rq_send.at[k, 1], rq_recv.at[k, 1], sib))

    def add_sibling(k):
        for c in to_sibling(k):
            c.wait_recv()
        part[k] = (part[k].astype(F32) + q_buf[k].astype(F32)).astype(BF16)
        pg_own[k] = pg_own[k] + qg_buf[k]

    def s_first(df):
        k = SLOT[(df, 2)]
        return (remote(part.at[k, 0], r1.at[df, 0], s1_send.at[df, 0], s1_recv.at[df, 0], s_up),
                remote(part.at[k, 1], r1.at[df, 1], s1_send.at[df, 1], s1_recv.at[df, 1], s_dn),
                remote(pg_own.at[k], r1g.at[df], s1_send.at[df, 2], s1_recv.at[df, 2], s_up))

    row = lax.broadcasted_iota(jnp.int32, (n_exp, loc), 0)
    col = lax.broadcasted_iota(jnp.int32, (n_exp, loc), 1)
    pick = jnp.where(row == ep * n_loc + lax.div(col, width), 1.0, 0.0).astype(F32)

    def widen(g):
        return lax.dot_general(g, pick, (((0,), (0,)), ((), ())), precision=lax.Precision.HIGHEST, preferred_element_type=F32)

    def compute(k):
        h = jnp.concatenate([x_own[k, 0], x_sib[k, 0]], axis=0)
        dy = jnp.concatenate([x_own[k, 1], x_sib[k, 1]], axis=0)
        gate = jnp.concatenate([widen(g_own[k]), widen(g_sib[k])], axis=0)
        both = jnp.dot(h, wgu[...], preferred_element_type=F32)
        g_pre = both[:, :loc]
        u_pre = both[:, loc:]
        d_raw = dot_nt(dy, wd[...])
        used = gate != 0.0
        sig = jax.nn.sigmoid(g_pre)
        silu = g_pre * sig
        act = (silu * u_pre).astype(BF16).astype(F32)
        act_g = jnp.where(used, gate * act, 0.0).astype(BF16)
        prod = jnp.where(used, act * d_raw, 0.0)
        d_act = gate * d_raw
        d_g = jnp.where(used, d_act * u_pre * sig * (1.0 + g_pre * (1.0 - sig)), 0.0).astype(BF16)
        d_u = jnp.where(used, d_act * silu, 0.0).astype(BF16)
        d_gu = jnp.concatenate([d_g, d_u], axis=1)
        prod_hi = prod.astype(BF16)
        prod_lo = (prod - prod_hi.astype(F32)).astype(BF16)
        pick_b = pick.astype(BF16)
        dgate = dot_nt(pick_b, prod_hi) + dot_nt(pick_b, prod_lo)
        pg_own[k] = dgate[:, :n_tok]
        pg_sib[k] = dgate[:, n_tok:]
        acc_b[...] += jnp.sum(dy.astype(F32).reshape(2 * n_tok // 8, 8, d_model), axis=0)
        acc_gu[...] += jnp.dot(h.T, d_gu, preferred_element_type=F32)
        acc_d[...] += jnp.dot(act_g.T, dy, preferred_element_type=F32)
        y = jnp.dot(act_g, wd[...], preferred_element_type=F32).astype(BF16)
        part[k, 0] = y[:n_tok]
        x_sib[k, 0] = y[n_tok:]
        dh = dot_nt(d_gu, wgu[...]).astype(BF16)
        part[k, 1] = dh[:n_tok]
        x_sib[k, 1] = dh[n_tok:]

    arrive(0)
    acc_gu[...] = jnp.zeros_like(acc_gu)
    acc_d[...] = jnp.zeros_like(acc_d)
    acc_b[...] = jnp.zeros_like(acc_b)
    for c in loads:
        c.wait()

    def step(k, carry):
        for j in range(N_SLOT - 1):
            @pl.when(k == j)
            def _():
                arrive(j + 1)
        remote(x_own.at[k], x_sib.at[k], ag_send.at[0], sib_recv.at[k, 0], sib).wait_recv()
        remote(g_own.at[k], g_sib.at[k], ag_send.at[0], sib_recv.at[k, 1], sib).wait_recv()
        compute(k)
        for c in to_sibling(k):
            c.start()

        @pl.when(k >= LAG)
        def _():
            add_sibling(k - LAG)
        for j, (df, ds) in enumerate(ORDER[:N_SLOT - LAG]):
            if ds == 2:
                @pl.when(k == j + LAG)
                def _():
                    for c in s_first(df):
                        c.start()
        return carry

    lax.fori_loop(0, N_SLOT, step, 0)

    stores = []
    for e in range(n_loc):
        cols = pl.ds(e * width, width)
        stores.append(pltpu.make_async_copy(acc_gu.at[:, cols], dwg_ref.at[e], load_sem.at[len(stores)]))
        stores.append(pltpu.make_async_copy(acc_gu.at[:, pl.ds(loc + e * width, width)], dwu_ref.at[e], load_sem.at[len(stores)]))
        stores.append(pltpu.make_async_copy(acc_d.at[cols], dwd_ref.at[e], load_sem.at[len(stores)]))
    for c in stores:
        c.start()
    dbias_ref[...] = acc_b[...]

    for j in range(N_SLOT - LAG, N_SLOT):
        add_sibling(j)
        df, ds = ORDER[j]
        if ds == 2:
            for c in s_first(df):
                c.start()

    def s_second(df, i):
        k = SLOT[(df, (1, 3)[i])]
        dev = (s_up, s_dn)[i]
        return (remote(part.at[k], r2.at[df, i], s2_send.at[df, i, 0], s2_recv.at[df, i, 0], dev),
                remote(pg_own.at[k], r2g.at[df, i], s2_send.at[df, i, 1], s2_recv.at[df, i, 1], dev))

    def add_into(k, t, block):
        part[k, t] = (part[k, t].astype(F32) + block[...].astype(F32)).astype(BF16)

    for df in (0, 1, 3, 2):
        for c in s_first(df):
            c.wait_recv()
        k = SLOT[(df, 1)]
        add_into(k, 0, r1.at[df, 0])
        pg_own[k] = pg_own[k] + r1g[df]
        add_into(SLOT[(df, 3)], 1, r1.at[df, 1])
        for i in range(2):
            for c in s_second(df, i):
                c.start()

    k2, k1, k3 = SLOT[(2, 0)], SLOT[(1, 0)], SLOT[(3, 0)]

    def wait_second(df):
        for i in range(2):
            for c in s_second(df, i):
                c.wait_recv()
        pg_own[SLOT[(df, 0)]] = pg_own[SLOT[(df, 0)]] + r2g[df, 0] + r2g[df, 1]

    def total(k, df, t):
        return part[k, t].astype(F32) + r2[df, 0, t].astype(F32) + r2[df, 1, t].astype(F32)

    f_first = (remote(part.at[k2, 0], r3.at[0], f1_send.at[0], f1_recv.at[0], f_up),
               remote(part.at[k2, 1], r3.at[1], f1_send.at[1], f1_recv.at[1], f_dn),
               remote(pg_own.at[k2], r3g, f1_send.at[2], f1_recv.at[2], f_up))
    f_second = (remote(part.at[k1], r4.at[0], f2_send.at[0], f2_recv.at[0], f_up),
                remote(pg_own.at[k1], r4g.at[0], f2_send.at[1], f2_recv.at[1], f_up),
                remote(part.at[k3], r4.at[1], f2_send.at[2], f2_recv.at[2], f_dn),
                remote(pg_own.at[k3], r4g.at[1], f2_send.at[3], f2_recv.at[3], f_dn))
    wait_second(1)
    part[k1, 0] = total(k1, 1, 0).astype(BF16)
    part[k1, 1] = total(k1, 1, 1).astype(BF16)
    wait_second(3)
    part[k3, 0] = total(k3, 3, 0).astype(BF16)
    part[k3, 1] = total(k3, 3, 1).astype(BF16)
    wait_second(0)
    ysum_ref[...] = total(0, 0, 0)
    dhsum_ref[...] = total(0, 0, 1)
    wait_second(2)
    part[k2, 0] = total(k2, 2, 0).astype(BF16)
    part[k2, 1] = total(k2, 2, 1).astype(BF16)
    for c in f_first:
        c.start()
    for c in f_first:
        c.wait_recv()
    add_into(k1, 0, r3.at[0])
    pg_own[k1] = pg_own[k1] + r3g[...]
    add_into(k3, 1, r3.at[1])
    for c in f_second:
        c.start()
    for c in f_second:
        c.wait_recv()
    ysum_ref[...] = ysum_ref[...] + r4[0, 0].astype(F32) + r4[1, 0].astype(F32)
    dhsum_ref[...] = dhsum_ref[...] + r4[0, 1].astype(F32) + r4[1, 1].astype(F32)
    dgate_ref[...] = pg_own[0] + r4g[0] + r4g[1]

    for c in stores:
        c.wait()
    for k in range(N_SLOT):
        for make in sends[k]:
            make().wait_send()
        for c in to_sibling(k):
            c.wait_send()
    for df in range(4):
        for c in s_first(df):
            c.wait_send()
        for i in range(2):
            for c in s_second(df, i):
                c.wait_send()
    for c in f_first + f_second:
        c.wait_send()


def moe(h, dy, gate_t, w_gate, w_up, w_down):
    n_tok, d_model = h.shape
    n_loc, _, width = w_gate.shape
    n_exp = gate_t.shape[0]
    loc = n_loc * width
    vmem = pl.BlockSpec(memory_space=pltpu.VMEM)
    hbm = pl.BlockSpec(memory_space=pl.ANY)
    block = (2, n_tok, d_model)
    small = (n_exp, n_tok)
    dma = pltpu.SemaphoreType.DMA
    scratch = [
        pltpu.VMEM((N_SLOT, *block), BF16), pltpu.VMEM((N_SLOT, *block), BF16), pltpu.VMEM((N_SLOT, *block), BF16),
        pltpu.VMEM((N_SLOT, *small), F32), pltpu.VMEM((N_SLOT, *small), F32),
        pltpu.VMEM((N_SLOT, *small), F32), pltpu.VMEM((N_SLOT, *small), F32),
        pltpu.VMEM((N_SLOT, *block), BF16), pltpu.VMEM((N_SLOT, *small), F32),
        pltpu.VMEM((4, *block), BF16), pltpu.VMEM((4, *small), F32),
        pltpu.VMEM((4, 2, *block), BF16), pltpu.VMEM((4, 2, *small), F32),
        pltpu.VMEM(block, BF16), pltpu.VMEM(small, F32),
        pltpu.VMEM((2, *block), BF16), pltpu.VMEM((2, *small), F32),
        pltpu.VMEM((d_model, 2 * loc), BF16), pltpu.VMEM((loc, d_model), BF16),
        pltpu.VMEM((d_model, 2 * loc), F32), pltpu.VMEM((loc, d_model), F32), pltpu.VMEM((8, d_model), F32),
        dma((3 * n_loc,)), dma((N_SEND,)), dma((N_SLOT, 2)), dma((N_SLOT,)), dma((N_SLOT, 2)),
        dma((N_SLOT, 2)), dma((N_SLOT, 2)), dma((4, 3)), dma((4, 3)), dma((4, 2, 2)), dma((4, 2, 2)),
        dma((3,)), dma((3,)), dma((4,)), dma((4,)),
    ]
    out_shape = (
        jax.ShapeDtypeStruct((n_tok, d_model), F32), jax.ShapeDtypeStruct((n_tok, d_model), F32),
        jax.ShapeDtypeStruct(small, F32), jax.ShapeDtypeStruct((8, d_model), F32),
        jax.ShapeDtypeStruct(w_gate.shape, F32), jax.ShapeDtypeStruct(w_up.shape, F32), jax.ShapeDtypeStruct(w_down.shape, F32),
    )
    return pl.pallas_call(
        moe_kernel, name="moe", out_shape=out_shape,
        in_specs=[vmem, vmem, vmem, hbm, hbm, hbm], out_specs=(vmem, vmem, vmem, vmem, hbm, hbm, hbm),
        scratch_shapes=scratch,
        compiler_params=pltpu.CompilerParams(collective_id=0, has_side_effects=True, vmem_limit_bytes=67_043_328),
    )(h, dy, gate_t, w_gate, w_up, w_down)


def solution(mesh):
    tok_spec = P(("dp", "ep", "tp"), None)
    wide_spec = P("ep", None, "tp")
    down_spec = P("ep", "tp", None)
    grad_wide = P(("dp", "ep"), None, "tp")
    grad_down = P(("dp", "ep"), "tp", None)

    def device_step(x_in, norm_gain, w_router, expert_idx, w_gate, w_up, w_down, out_bias, dy_out):
        n_exp = w_router.shape[1]
        x_f32 = x_in.astype(F32)
        inv_rms = lax.rsqrt(jnp.mean(x_f32 * x_f32, axis=-1, keepdims=True) + EPS)
        normed = x_f32 * inv_rms
        gain_f32 = norm_gain.astype(F32)
        hidden = (normed * gain_f32).astype(BF16)
        logits = jnp.dot(hidden, w_router, preferred_element_type=F32)
        chosen = jnp.any(expert_idx[:, :, None] == jnp.arange(n_exp)[None, None, :], axis=1)
        gates = jax.nn.softmax(jnp.where(chosen, logits, -jnp.inf), axis=-1)
        y_sum, dh_sum, dgate_t, dbias_8, d_gate, d_up, d_down = moe(hidden, dy_out, gates.T, w_gate, w_up, w_down)
        d_gates = jnp.where(chosen, dgate_t.T, 0.0)
        y_out = (x_f32 + (y_sum + out_bias.astype(F32))).astype(BF16)
        dy_f32 = dy_out.astype(F32)
        d_logits = gates * (d_gates - jnp.sum(gates * d_gates, axis=-1, keepdims=True))
        d_router = jnp.einsum("td,te->de", hidden, d_logits, preferred_element_type=F32)
        dh_total = dh_sum + jnp.einsum("te,de->td", d_logits, w_router, preferred_element_type=F32)
        d_gain = jnp.sum(dh_total * normed, axis=0)
        d_norm = dh_total * gain_f32
        dx_in = (dy_f32 + inv_rms * (d_norm - normed * jnp.mean(d_norm * normed, axis=-1, keepdims=True))).astype(BF16)
        d_gain, d_router = lax.psum((d_gain, d_router), ("ep", "tp"))
        return y_out, dx_in, d_gain, d_router, d_gate, d_up, d_down, jnp.sum(dbias_8, axis=0)

    return jax.shard_map(device_step, mesh=mesh, in_specs=(tok_spec, P(None), P(None, None), tok_spec, wide_spec, wide_spec, down_spec, P(None), tok_spec), out_specs=(tok_spec, tok_spec, P("dp"), P("dp", None), grad_wide, grad_wide, grad_down, P("dp")), check_vma=False)
```

time: 1260 us -> 262 us (0.21)
  waiting for transfers between devices: 834 us -> 41.9 us
  Pallas kernels: 0 us -> 138 us
  matrix products: 113 us -> 4.52 us
  blocking collectives: 153 us -> 45.3 us
  local copies, waits for them, and re-layouts: 90.1 us -> 9.37 us
  other arithmetic: 43.7 us -> 8.24 us
    unnamed x5 -> x1, waiting for transfers between devices: 560 us -> 0.05 us
    all_gather x2 -> x0, waiting for transfers between devices: 220 us -> none  [the longest x1 121 us: device_step(): d_rows = lax.all_gather(d_recv, 'tp', axis=0)]
    pallas_call x0 -> x1, Pallas kernels: none -> 138 us  [moe(): pl.pallas_call(moe_kernel, name='moe', out_shape=out_shape, in_specs=[vme...]
    all_to_all x2 -> x0, blocking collectives: 108 us -> none  [the longest x1 54.4 us: device_step(): recv_rows = lax.all_to_all(send_rows, 'ep', 0, 0, tiled=True)]
    dot_general x12 -> x3, matrix products: 113 us -> 4.52 us  [the longest x1 1.81 us: device_step(): jnp.einsum('td,te->de', hidden, d_logits, preferred_element_type=F32)]
    gather x8 -> x0, local copies, waits for them, and re-layouts: 45.2 us -> none  [the longest x1 9.67 us: device_step(): dy_copy[slot_copy]]
    all_gather x2 -> x0, local copies, waits for them, and re-layouts: 28.2 us -> none  [the longest x1 14.1 us: device_step(): rows_in = lax.all_gather(recv_rows, 'tp', axis=0)]
    all_to_all x2 -> x0, waiting for transfers between devices: 21.6 us -> none  [the longest x1 16.7 us: device_step(): lax.all_to_all(y_recv, 'ep', 0, 0, tiled=True)]
  transfers between devices with their start and end apart: 6 -> 1, of which waited for: 6 -> 1; matrix products, arithmetic and copies ran while one was open for 10% -> 2% of each run, Pallas kernels for 0% -> 0%
where the time goes in v1:
time: 262 us
  Pallas kernels  138 us (53%)
  blocking collectives  45.3 us (17%)
  waiting for transfers between devices  41.9 us (16%)
  between operations  14.2 us (5%)
  local copies, waits for them, and re-layouts  9.37 us (4%)
  other arithmetic  8.24 us (3%)
  matrix products  4.52 us (2%)
    pallas_call x1, Pallas kernels, moe(): pl.pallas_call(moe_kernel, name='moe', out_shape=out_shape, in_specs=[vme...  138 us
    psum x1, blocking collectives, device_step(): d_gain, d_router = lax.psum((d_gain, d_router), ('ep', 'tp'))  45.3 us
    psum x1, waiting for transfers between devices, device_step(): d_gain, d_router = lax.psum((d_gain, d_router), ('ep', 'tp'))  41.9 us
    unnamed x32, local copies, waits for them, and re-layouts  9.37 us
  transfers between devices with their start and end apart: 1, of which 1 were waited for; matrix products, arithmetic and copies ran while one was open for 2% of the time, Pallas kernels for 0%

profile of v1, /device:TPU:97, one launch (start us, length us, event | category | flops | bytes accessed | tf_op | source)
XLA Modules:
  0.0 261.7 jit_solution(5684914272299082196)
XLA Ops:
  7.2 0.1 all-reduce.2.cloned.1.call-start
  7.2 1.1 fusion.11
  8.3 0.0 copy-start.13
  8.3 0.7 fusion.13
  9.1 0.0 copy-start.8
  9.1 0.7 convert_element_type.22
  9.8 0.0 copy-start.9
  9.8 1.1 fusion.4.h_ref
  10.8 0.0 copy-start
  10.9 0.7 copy-done
  11.6 1.0 fusion.22
  12.6 0.0 copy-done.8
  12.6 0.0 copy-start.6
  12.6 0.0 copy-start.11
  12.6 0.0 copy-done.9
  12.7 0.0 copy-done.13
  12.7 0.5 copy-done.6
  13.2 0.0 copy-done.11
  13.2 0.0 copy-start.12
  13.2 0.5 copy-done.12
  13.7 0.6 fusion.21.gate_ref
  14.4 138.1 %moe.1 = (f32[128,1024]{1,0:T(8,128)}, f32[128,1024]{1,0:T(8,128)}, f32[32,128]{1,0:T(8,128)}, f32[8,1024]{1,0:T(8,128)}, f32[4,1024,128]{2,1,0:T(8,128)}, /*ind...) custom-call(bf16[128,1024]{1,0:T(8,128)(2,1)} %copy-done, bf16[128,1024]{1,0:T(8,128)(2,1)} %dy_ref.1, ...), custom_call_target="tpu_custom_call" | custom-call | tf_op jit(solution)/shard_map/moe/pallas_call | solution.py:335
  152.4 0.0 copy-start.1
  152.4 0.0 copy-start.5
  152.5 0.0 copy-start.7
  152.5 0.0 copy-start.10
  152.5 0.8 multiply_reduce_fusion
  153.3 1.8 fusion.16
  155.1 0.0 copy-start.4
  155.1 0.1 all-reduce.2.cloned.1.call-update
  155.2 0.8 convert_element_type.24
  156.0 1.7 fusion.10
  157.7 0.0 copy-done.1
  157.7 0.0 copy-done.5
  157.7 0.0 copy-done.7
  157.7 1.8 fusion.9
  159.5 0.0 copy-done.10
  159.5 0.6 reduce_sum.59
  160.1 45.3 %psum.14 = f32[1024]{0:T(1024)} all-reduce(f32[1024]{0:T(1024)S(1)} %get-tuple-element.22), channel_id=1, replica_groups=mesh['dp'=1,'tp'=4,'ep'=8] {'ep','tp'}, use_global_device_ids=true, to_apply=%region_7.8 | all-reduce | flops 1024 | bytes 8192 | tf_op jit(solution)/shard_map/psum | solution.py:370
  205.4 41.9 %all-reduce.2.cloned.1.call-done = f32[1024,32]{0,1:T(8,128)} async-done(((f32[1024,32]{0,1:T(8,128)}), f32[1024,32]{0,1:T(8,128)}) %all-reduce.2.cloned.1.call-update) | async-done | bytes 131088 | tf_op jit(solution)/shard_map/psum | solution.py:370
  247.2 1.6 copy.22
  248.8 0.0 copy-done.4
  248.8 1.3 copy.23
  250.1 1.0 copy-done.3
  251.2 0.0 copy-start.2
  251.2 1.3 copy.24
  252.5 1.0 copy-done.2
  253.5 1.3 copy.25
  (4 shorter events, 0.0 us)
Async XLA Ops:
  7.2 240.1 %all-reduce.2.cloned.1.call-start = ((), (), s32[]{:S(2)}) async-start(), calls=%async_computation | async-start | bytes 262144 | tf_op jit(solution)/shard_map/psum | solution.py:370
  8.3 4.3 %copy-start.13 = (f32[128]{0:T(128)}, f32[128]{0:T(128)S(1)}, u32[]{:S(2)}) copy-start(f32[128]{0:T(128)S(1)} %add_rsqrt_fusion) | copy-start | bytes 1540
  9.1 3.5 %copy-start.8 = (pred[128,32]{0,1:T(8,128)(4,1)}, pred[128,32]{0,1:T(8,128)(4,1)S(1)}, u32[]{:S(2)}) copy-start(pred[128,32]{0,1:T(8,128)(4,1)S(1)} %fusion.13) | copy-start | bytes 12292
  9.8 2.9 %copy-start.9 = (f32[1024]{0:T(1024)}, f32[1024]{0:T(1024)S(1)}, u32[]{:S(2)}) copy-start(f32[1024]{0:T(1024)S(1)} %convert_element_type.22) | copy-start | bytes 12292
  10.8 0.7 copy-start
  12.6 0.6 copy-start.6
  12.6 0.6 copy-start.11
  13.2 0.5 copy-start.12
  152.4 5.3 %copy-start.1 = (bf16[128,1024]{1,0:T(8,128)(2,1)S(1)}, bf16[128,1024]{1,0:T(8,128)(2,1)}, u32[]{:S(2)}) copy-start(bf16[128,1024]{1,0:T(8,128)(2,1)} %param.9) | copy-start | bytes 786436
  152.4 5.3 %copy-start.5 = (bf16[128,1024]{1,0:T(8,128)(2,1)S(1)}, bf16[128,1024]{1,0:T(8,128)(2,1)}, u32[]{:S(2)}) copy-start(bf16[128,1024]{1,0:T(8,128)(2,1)} %dy_ref.1) | copy-start | bytes 786436
  152.5 5.3 %copy-start.7 = (f32[128,1024]{1,0:T(8,128)S(1)}, f32[128,1024]{1,0:T(8,128)}, u32[]{:S(2)}) copy-start(f32[128,1024]{1,0:T(8,128)} %get-tuple-element.15) | copy-start | bytes 1572868
  152.5 7.0 %copy-start.10 = (f32[8,1024]{1,0:T(8,128)S(1)}, f32[8,1024]{1,0:T(8,128)}, u32[]{:S(2)}) copy-start(f32[8,1024]{1,0:T(8,128)} %get-tuple-element.21) | copy-start | bytes 98308
  155.1 93.7 %copy-start.4 = (f32[4,1024,128]{2,1,0:T(8,128)S(1)}, f32[4,1024,128]{2,1,0:T(8,128)}, u32[]{:S(2)}) copy-start(f32[4,1024,128]{2,1,0:T(8,128)} %get-tuple-element.41) | copy-start | bytes 6291460
  248.8 2.3 copy-start.3
  251.2 2.3 copy-start.2
Sparse Core Ops, SparseCore 0:
  155.3 91.8 all-reduce.1

commit v2 on v1

--- a/solution.py
+++ b/solution.py
@@ -9,23 +9,27 @@
 MESH = pl.DeviceIdType.MESH
 F32 = jnp.float32
 BF16 = jnp.bfloat16
-ORDER = ((0, 0), (1, 0), (3, 0), (0, 1), (0, 3), (2, 0), (0, 2), (1, 1), (1, 3), (1, 2), (3, 1), (3, 3), (3, 2), (2, 1), (2, 3), (2, 2))
+ORDER = ((0, 0), (0, 1), (0, 3), (0, 2), (1, 0), (1, 1), (1, 3), (3, 1), (3, 3), (1, 2), (2, 1), (2, 3), (3, 2), (2, 2), (2, 0), (3, 0))
+ARRIVALS = {1: ((0, 1), (0, 3), (1, 0), (3, 0)), 2: ((2, 0), (0, 2)), 4: ((1, 1), (1, 3)), 6: ((3, 1), (3, 3)),
+            8: ((1, 2),), 9: ((2, 1), (2, 3)), 11: ((3, 2),), 12: ((2, 2),)}
+FIRST_AT = {4: 0, 10: 1, 13: 3, 14: 2}
+SECOND_AT = {6: 0, 12: 1, 15: 3}
 SLOT = {place: k for k, place in enumerate(ORDER)}
 N_SLOT = len(ORDER)
 N_SEND = 67
-LAG = 2
+LAG = 1
 
 
 def dot_nt(a, b):
     return lax.dot_general(a, b, (((1,), (1,)), ((), ())), preferred_element_type=F32)
 
 
-def moe_kernel(h_ref, dy_ref, gate_ref, wg_ref, wu_ref, wd_ref,
-               ysum_ref, dhsum_ref, dgate_ref, dbias_ref, dwg_ref, dwu_ref, dwd_ref,
+def moe_kernel(x_ref, dy_ref, idx_ref, gain_ref, bias_ref, router_ref, wg_ref, wu_ref, wd_ref,
+               y_ref, dx_ref, dgain_ref, drouter_ref, dbias_ref, dwg_ref, dwu_ref, dwd_ref,
                x_own, x_sib, part, g_own, g_sib, pg_own, pg_sib, q_buf, qg_buf,
-               r1, r1g, r2, r2g, r3, r3g, r4, r4g, wgu, wd, acc_gu, acc_d, acc_b,
+               r1, r1g, r2, r2g, r3, r3g, r4, r4g, dl_buf, dr_buf, gn_buf, wgu, wd, acc_gu, acc_d, acc_b,
                load_sem, ag_send, ag_recv, ag_grecv, sib_recv,
-               rq_send, rq_recv, s1_send, s1_recv, s2_send, s2_recv, f1_send, f1_recv, f2_send, f2_recv):
+               rq_send, rq_recv, s1_send, s1_recv, s2_send, s2_recv, f1_send, f1_recv, f2_send, f2_recv, e_send, e_recv):
     ep = lax.axis_index("ep")
     tp = lax.axis_index("tp")
     n_tp = lax.axis_size("tp")
@@ -33,8 +37,8 @@
     core = lax.rem(ep, 2)
     chip_x = lax.div(ep, 2)
     n_loc, d_model, width = wg_ref.shape
-    n_tok = h_ref.shape[0]
-    n_exp = gate_ref.shape[0]
+    n_tok = x_ref.shape[0]
+    n_exp = router_ref.shape[0]
     loc = n_loc * width
 
     def shifted(x_step, y_step):
@@ -46,6 +50,8 @@
     f_dn = shifted(core - 1, -core)
     s_up = shifted(core, 1 - core)
     s_dn = shifted(-core, core - 1)
+    f_op = shifted(2 * (1 - core), 2 * core)
+    s_op = shifted(2 * core, 2 * (1 - core))
     sib = {"ep": ep + 1 - 2 * core}
 
     loads = []
@@ -56,14 +62,31 @@
         loads.append(pltpu.make_async_copy(wd_ref.at[e], wd.at[cols], load_sem.at[len(loads)]))
     for c in loads:
         c.start()
-    x_own[0, 0] = h_ref[...]
+    barrier = pltpu.get_barrier_semaphore()
+    peers = (f_up, f_dn, f_op, s_up, s_dn, s_op, sib)
+    for dev in peers:
+        pl.semaphore_signal(barrier, inc=1, device_id=dev, device_id_type=MESH)
+
+    def normalised():
+        x = x_ref[...].astype(F32)
+        inv_rms = lax.rsqrt(jnp.mean(x * x, axis=-1, keepdims=True) + EPS)
+        return x, inv_rms, x * inv_rms
+
+    def chosen_mask():
+        expert = lax.broadcasted_iota(jnp.int32, (n_exp, n_tok), 0)
+        chosen = expert == idx_ref[0:1, :]
+        for j in range(1, idx_ref.shape[0]):
+            chosen = jnp.logical_or(chosen, expert == idx_ref[j:j + 1, :])
+        return chosen
+
+    gain = gain_ref[...].astype(F32)
+    hidden = (normalised()[2] * gain).astype(BF16)
+    x_own[0, 0] = hidden
     x_own[0, 1] = dy_ref[...]
-    g_own[0] = gate_ref[...]
-
-    barrier = pltpu.get_barrier_semaphore()
-    for dev in (f_up, f_dn, s_up, s_dn, sib):
-        pl.semaphore_signal(barrier, inc=1, device_id=dev, device_id_type=MESH)
-    pl.semaphore_wait(barrier, 5)
+    logits = jnp.where(chosen_mask(), dot_nt(router_ref[...], hidden), -jnp.inf)
+    weight = jnp.exp(logits - jnp.max(logits, axis=0, keepdims=True))
+    g_own[0] = weight / jnp.sum(weight, axis=0, keepdims=True)
+    pl.semaphore_wait(barrier, len(peers))
 
     def remote(src, dst, send, recv, dev):
         return pltpu.make_async_remote_copy(src_ref=src, dst_ref=dst, send_sem=send, recv_sem=recv, device_id=dev, device_id_type=MESH)
@@ -130,6 +153,26 @@
         return (remote(part.at[k, 0], r1.at[df, 0], s1_send.at[df, 0], s1_recv.at[df, 0], s_up),
                 remote(part.at[k, 1], r1.at[df, 1], s1_send.at[df, 1], s1_recv.at[df, 1], s_dn),
                 remote(pg_own.at[k], r1g.at[df], s1_send.at[df, 2], s1_recv.at[df, 2], s_up))
+
+    def s_second(df, i):
+        k = SLOT[(df, (1, 3)[i])]
+        dev = (s_up, s_dn)[i]
+        return (remote(pg_own.at[k], r2g.at[df, i], s2_send.at[df, i, 1], s2_recv.at[df, i, 1], dev),
+                remote(part.at[k], r2.at[df, i], s2_send.at[df, i, 0], s2_recv.at[df, i, 0], dev))
+
+    def add_into(k, t, block):
+        part[k, t] = (part[k, t].astype(F32) + block[...].astype(F32)).astype(BF16)
+
+    def send_second(df):
+        for c in s_first(df):
+            c.wait_recv()
+        k = SLOT[(df, 1)]
+        add_into(k, 0, r1.at[df, 0])
+        pg_own[k] = pg_own[k] + r1g[df]
+        add_into(SLOT[(df, 3)], 1, r1.at[df, 1])
+        for i in range(2):
+            for c in s_second(df, i):
+                c.start()
 
     row = lax.broadcasted_iota(jnp.int32, (n_exp, loc), 0)
     col = lax.broadcasted_iota(jnp.int32, (n_exp, loc), 1)
@@ -180,10 +223,11 @@
         c.wait()
 
     def step(k, carry):
-        for j in range(N_SLOT - 1):
+        for j, places in ARRIVALS.items():
             @pl.when(k == j)
             def _():
-                arrive(j + 1)
+                for place in places:
+                    arrive(SLOT[place])
         remote(x_own.at[k], x_sib.at[k], ag_send.at[0], sib_recv.at[k, 0], sib).wait_recv()
         remote(g_own.at[k], g_sib.at[k], ag_send.at[0], sib_recv.at[k, 1], sib).wait_recv()
         compute(k)
@@ -193,12 +237,15 @@
         @pl.when(k >= LAG)
         def _():
             add_sibling(k - LAG)
-        for j, (df, ds) in enumerate(ORDER[:N_SLOT - LAG]):
-            if ds == 2:
-                @pl.when(k == j + LAG)
-                def _():
-                    for c in s_first(df):
-                        c.start()
+        for j, df in FIRST_AT.items():
+            @pl.when(k == j)
+            def _():
+                for c in s_first(df):
+                    c.start()
+        for j, df in SECOND_AT.items():
+            @pl.when(k == j)
+            def _():
+                send_second(df)
         return carry
 
     lax.fori_loop(0, N_SLOT, step, 0)
@@ -211,34 +258,10 @@
         stores.append(pltpu.make_async_copy(acc_d.at[cols], dwd_ref.at[e], load_sem.at[len(stores)]))
     for c in stores:
         c.start()
-    dbias_ref[...] = acc_b[...]
-
+    dbias_ref[...] = jnp.sum(acc_b[...], axis=0, keepdims=True)
     for j in range(N_SLOT - LAG, N_SLOT):
         add_sibling(j)
-        df, ds = ORDER[j]
-        if ds == 2:
-            for c in s_first(df):
-                c.start()
-
-    def s_second(df, i):
-        k = SLOT[(df, (1, 3)[i])]
-        dev = (s_up, s_dn)[i]
-        return (remote(part.at[k], r2.at[df, i], s2_send.at[df, i, 0], s2_recv.at[df, i, 0], dev),
-                remote(pg_own.at[k], r2g.at[df, i], s2_send.at[df, i, 1], s2_recv.at[df, i, 1], dev))
-
-    def add_into(k, t, block):
-        part[k, t] = (part[k, t].astype(F32) + block[...].astype(F32)).astype(BF16)
-
-    for df in (0, 1, 3, 2):
-        for c in s_first(df):
-            c.wait_recv()
-        k = SLOT[(df, 1)]
-        add_into(k, 0, r1.at[df, 0])
-        pg_own[k] = pg_own[k] + r1g[df]
-        add_into(SLOT[(df, 3)], 1, r1.at[df, 1])
-        for i in range(2):
-            for c in s_second(df, i):
-                c.start()
+    send_second(2)
 
     k2, k1, k3 = SLOT[(2, 0)], SLOT[(1, 0)], SLOT[(3, 0)]
 
@@ -251,40 +274,89 @@
     def total(k, df, t):
         return part[k, t].astype(F32) + r2[df, 0, t].astype(F32) + r2[df, 1, t].astype(F32)
 
-    f_first = (remote(part.at[k2, 0], r3.at[0], f1_send.at[0], f1_recv.at[0], f_up),
-               remote(part.at[k2, 1], r3.at[1], f1_send.at[1], f1_recv.at[1], f_dn),
-               remote(pg_own.at[k2], r3g, f1_send.at[2], f1_recv.at[2], f_up))
-    f_second = (remote(part.at[k1], r4.at[0], f2_send.at[0], f2_recv.at[0], f_up),
-                remote(pg_own.at[k1], r4g.at[0], f2_send.at[1], f2_recv.at[1], f_up),
-                remote(part.at[k3], r4.at[1], f2_send.at[2], f2_recv.at[2], f_dn),
-                remote(pg_own.at[k3], r4g.at[1], f2_send.at[3], f2_recv.at[3], f_dn))
-    wait_second(1)
-    part[k1, 0] = total(k1, 1, 0).astype(BF16)
-    part[k1, 1] = total(k1, 1, 1).astype(BF16)
-    wait_second(3)
-    part[k3, 0] = total(k3, 3, 0).astype(BF16)
-    part[k3, 1] = total(k3, 3, 1).astype(BF16)
-    wait_second(0)
-    ysum_ref[...] = total(0, 0, 0)
-    dhsum_ref[...] = total(0, 0, 1)
-    wait_second(2)
-    part[k2, 0] = total(k2, 2, 0).astype(BF16)
-    part[k2, 1] = total(k2, 2, 1).astype(BF16)
+    f_first = (remote(pg_own.at[k2], r3g, f1_send.at[2], f1_recv.at[2], f_up),
+               remote(part.at[k2, 0], r3.at[0], f1_send.at[0], f1_recv.at[0], f_up),
+               remote(part.at[k2, 1], r3.at[1], f1_send.at[1], f1_recv.at[1], f_dn))
+    f_second = (remote(pg_own.at[k1], r4g.at[0], f2_send.at[1], f2_recv.at[1], f_up),
+                remote(pg_own.at[k3], r4g.at[1], f2_send.at[3], f2_recv.at[3], f_dn),
+                remote(part.at[k1], r4.at[0], f2_send.at[0], f2_recv.at[0], f_up),
+                remote(part.at[k3], r4.at[1], f2_send.at[2], f2_recv.at[2], f_dn))
+    for df, k in ((1, k1), (3, k3), (0, 0), (2, k2)):
+        wait_second(df)
+        if df:
+            part[k, 0] = total(k, df, 0).astype(BF16)
+            part[k, 1] = total(k, df, 1).astype(BF16)
     for c in f_first:
         c.start()
     for c in f_first:
         c.wait_recv()
+    pg_own[k1] = pg_own[k1] + r3g[...]
     add_into(k1, 0, r3.at[0])
-    pg_own[k1] = pg_own[k1] + r3g[...]
     add_into(k3, 1, r3.at[1])
     for c in f_second:
         c.start()
-    for c in f_second:
+
+    for c in f_second[:2]:
         c.wait_recv()
-    ysum_ref[...] = ysum_ref[...] + r4[0, 0].astype(F32) + r4[1, 0].astype(F32)
-    dhsum_ref[...] = dhsum_ref[...] + r4[0, 1].astype(F32) + r4[1, 1].astype(F32)
-    dgate_ref[...] = pg_own[0] + r4g[0] + r4g[1]
-
+    gates = g_own[0]
+    d_gates = jnp.where(chosen_mask(), pg_own[0] + r4g[0] + r4g[1], 0.0)
+    d_logits = gates * (d_gates - jnp.sum(gates * d_gates, axis=0, keepdims=True))
+    dl_buf[0, 0] = d_logits
+    dh_router = lax.dot_general(d_logits, router_ref[...].astype(F32), (((0,), (0,)), ((), ())), precision=lax.Precision.HIGHEST, preferred_element_type=F32)
+    f_dl = [remote(dl_buf.at[0, 0], dl_buf.at[0, to], e_send.at[i], e_recv.at[i], dev) for i, (to, dev) in enumerate(((3, f_up), (1, f_dn), (2, f_op)))]
+    s_dl = [remote(dl_buf.at[0], dl_buf.at[to], e_send.at[3 + i], e_recv.at[3 + i], dev) for i, (to, dev) in enumerate(((3, s_up), (1, s_dn), (2, s_op)))]
+    for c in f_dl:
+        c.start()
+    for c in f_dl:
+        c.wait_recv()
+    for c in s_dl:
+        c.start()
+    for c in s_dl:
+        c.wait_recv()
+    d_router = jnp.zeros((n_exp, d_model), F32)
+    for k, (df, ds) in enumerate(ORDER):
+        dl = dl_buf[ds, df]
+        dl_hi = dl.astype(BF16)
+        dl_lo = (dl - dl_hi.astype(F32)).astype(BF16)
+        prods = jnp.dot(jnp.concatenate([dl_hi, dl_lo], axis=0), x_own[k, 0], preferred_element_type=F32)
+        d_router = d_router + (prods[:n_exp] + prods[n_exp:])
+    dr_buf[0] = d_router
+
+    for c in f_second[2:]:
+        c.wait_recv()
+    sib_dr = remote(dr_buf.at[0], dr_buf.at[1], e_send.at[6], e_recv.at[6], sib)
+    sib_dr.start()
+    x, inv_rms, normed = normalised()
+    dh_total = total(0, 0, 1) + r4[0, 1].astype(F32) + r4[1, 1].astype(F32) + dh_router
+    gn_buf[0] = jnp.sum(dh_total * normed, axis=0, keepdims=True)
+    d_norm = dh_total * gain
+    dx_ref[...] = (dy_ref[...].astype(F32) + inv_rms * (d_norm - normed * jnp.mean(d_norm * normed, axis=-1, keepdims=True))).astype(BF16)
+    exchanges = [sib_dr]
+    n_sem = 7
+    for group in ((f_up, f_dn, f_op), (s_up, s_dn, s_op), (sib,)):
+        base = n_sem - 7
+        copies = [remote(gn_buf.at[base], gn_buf.at[base + 1 + i], e_send.at[n_sem + i], e_recv.at[n_sem + i], dev) for i, dev in enumerate(group)]
+        for c in copies:
+            c.start()
+        if base == 0:
+            y_moe = total(0, 0, 0) + r4[0, 0].astype(F32) + r4[1, 0].astype(F32)
+            y_ref[...] = (x + (y_moe + bias_ref[...].astype(F32))).astype(BF16)
+        for c in copies:
+            c.wait_recv()
+        summed = gn_buf[base]
+        for i in range(len(group)):
+            summed = summed + gn_buf[base + 1 + i]
+        exchanges += copies
+        n_sem += len(group) + 1
+        if len(group) > 1:
+            gn_buf[n_sem - 7] = summed
+        else:
+            dgain_ref[...] = summed
+    sib_dr.wait_recv()
+    drouter_ref[...] = dr_buf[0] + dr_buf[1]
+
+    for c in f_dl + s_dl + exchanges:
+        c.wait_send()
     for c in stores:
         c.wait()
     for k in range(N_SLOT):
@@ -302,10 +374,10 @@
         c.wait_send()
 
 
-def moe(h, dy, gate_t, w_gate, w_up, w_down):
-    n_tok, d_model = h.shape
+def moe(x, dy, idx_t, gain, bias, router_t, w_gate, w_up, w_down):
+    n_tok, d_model = x.shape
     n_loc, _, width = w_gate.shape
-    n_exp = gate_t.shape[0]
+    n_exp = router_t.shape[0]
     loc = n_loc * width
     vmem = pl.BlockSpec(memory_space=pltpu.VMEM)
     hbm = pl.BlockSpec(memory_space=pl.ANY)
@@ -321,23 +393,24 @@
         pltpu.VMEM((4, 2, *block), BF16), pltpu.VMEM((4, 2, *small), F32),
         pltpu.VMEM(block, BF16), pltpu.VMEM(small, F32),
         pltpu.VMEM((2, *block), BF16), pltpu.VMEM((2, *small), F32),
+        pltpu.VMEM((4, 4, *small), F32), pltpu.VMEM((2, n_exp, d_model), F32), pltpu.VMEM((10, 1, d_model), F32),
         pltpu.VMEM((d_model, 2 * loc), BF16), pltpu.VMEM((loc, d_model), BF16),
         pltpu.VMEM((d_model, 2 * loc), F32), pltpu.VMEM((loc, d_model), F32), pltpu.VMEM((8, d_model), F32),
         dma((3 * n_loc,)), dma((N_SEND,)), dma((N_SLOT, 2)), dma((N_SLOT,)), dma((N_SLOT, 2)),
         dma((N_SLOT, 2)), dma((N_SLOT, 2)), dma((4, 3)), dma((4, 3)), dma((4, 2, 2)), dma((4, 2, 2)),
-        dma((3,)), dma((3,)), dma((4,)), dma((4,)),
+        dma((3,)), dma((3,)), dma((4,)), dma((4,)), dma((17,)), dma((17,)),
     ]
     out_shape = (
-        jax.ShapeDtypeStruct((n_tok, d_model), F32), jax.ShapeDtypeStruct((n_tok, d_model), F32),
-        jax.ShapeDtypeStruct(small, F32), jax.ShapeDtypeStruct((8, d_model), F32),
+        jax.ShapeDtypeStruct((n_tok, d_model), BF16), jax.ShapeDtypeStruct((n_tok, d_model), BF16),
+        jax.ShapeDtypeStruct((1, d_model), F32), jax.ShapeDtypeStruct((n_exp, d_model), F32), jax.ShapeDtypeStruct((1, d_model), F32),
         jax.ShapeDtypeStruct(w_gate.shape, F32), jax.ShapeDtypeStruct(w_up.shape, F32), jax.ShapeDtypeStruct(w_down.shape, F32),
     )
     return pl.pallas_call(
         moe_kernel, name="moe", out_shape=out_shape,
-        in_specs=[vmem, vmem, vmem, hbm, hbm, hbm], out_specs=(vmem, vmem, vmem, vmem, hbm, hbm, hbm),
+        in_specs=[vmem] * 6 + [hbm] * 3, out_specs=(vmem,) * 5 + (hbm,) * 3,
         scratch_shapes=scratch,
         compiler_params=pltpu.CompilerParams(collective_id=0, has_side_effects=True, vmem_limit_bytes=67_043_328),
-    )(h, dy, gate_t, w_gate, w_up, w_down)
+    )(x, dy, idx_t, gain, bias, router_t, w_gate, w_up, w_down)
 
 
 def solution(mesh):
@@ -348,26 +421,8 @@
     grad_down = P(("dp", "ep"), "tp", None)
 
     def device_step(x_in, norm_gain, w_router, expert_idx, w_gate, w_up, w_down, out_bias, dy_out):
-        n_exp = w_router.shape[1]
-        x_f32 = x_in.astype(F32)
-        inv_rms = lax.rsqrt(jnp.mean(x_f32 * x_f32, axis=-1, keepdims=True) + EPS)
-        normed = x_f32 * inv_rms
-        gain_f32 = norm_gain.astype(F32)
-        hidden = (normed * gain_f32).astype(BF16)
-        logits = jnp.dot(hidden, w_router, preferred_element_type=F32)
-        chosen = jnp.any(expert_idx[:, :, None] == jnp.arange(n_exp)[None, None, :], axis=1)
-        gates = jax.nn.softmax(jnp.where(chosen, logits, -jnp.inf), axis=-1)
-        y_sum, dh_sum, dgate_t, dbias_8, d_gate, d_up, d_down = moe(hidden, dy_out, gates.T, w_gate, w_up, w_down)
-        d_gates = jnp.where(chosen, dgate_t.T, 0.0)
-        y_out = (x_f32 + (y_sum + out_bias.astype(F32))).astype(BF16)
-        dy_f32 = dy_out.astype(F32)
-        d_logits = gates * (d_gates - jnp.sum(gates * d_gates, axis=-1, keepdims=True))
-        d_router = jnp.einsum("td,te->de", hidden, d_logits, preferred_element_type=F32)
-        dh_total = dh_sum + jnp.einsum("te,de->td", d_logits, w_router, preferred_element_type=F32)
-        d_gain = jnp.sum(dh_total * normed, axis=0)
-        d_norm = dh_total * gain_f32
-        dx_in = (dy_f32 + inv_rms * (d_norm - normed * jnp.mean(d_norm * normed, axis=-1, keepdims=True))).astype(BF16)
-        d_gain, d_router = lax.psum((d_gain, d_router), ("ep", "tp"))
-        return y_out, dx_in, d_gain, d_router, d_gate, d_up, d_down, jnp.sum(dbias_8, axis=0)
+        y_out, dx_in, d_gain, d_router_t, d_bias, d_gate, d_up, d_down = moe(
+            x_in, dy_out, expert_idx.T, norm_gain[None, :], out_bias[None, :], w_router.T, w_gate, w_up, w_down)
+        return y_out, dx_in, d_gain[0], d_router_t.T, d_gate, d_up, d_down, d_bias[0]
 
     return jax.shard_map(device_step, mesh=mesh, in_specs=(tok_spec, P(None), P(None, None), tok_spec, wide_spec, wide_spec, down_spec, P(None), tok_spec), out_specs=(tok_spec, tok_spec, P("dp"), P("dp", None), grad_wide, grad_wide, grad_down, P("dp")), check_vma=False)

time: 262 us -> 155 us (0.59)
  blocking collectives: 45.3 us -> 0 us
  waiting for transfers between devices: 41.9 us -> 0 us
  between operations: 14.2 us -> 0.65 us
  other arithmetic: 8.24 us -> 0 us
  local copies, waits for them, and re-layouts: 9.37 us -> 16.2 us
  matrix products: 4.52 us -> 0 us
    psum x1 -> x0, blocking collectives: 45.3 us -> none  [device_step(): d_gain, d_router = lax.psum((d_gain, d_router), ('ep', 'tp'))]
    psum x1 -> x0, waiting for transfers between devices: 41.9 us -> none  [device_step(): d_gain, d_router = lax.psum((d_gain, d_router), ('ep', 'tp'))]
    dot_general x3 -> x0, matrix products: 4.52 us -> none  [the longest x1 1.81 us: device_step(): jnp.einsum('td,te->de', hidden, d_logits, preferred_element_type=F32)]
    convert_element_type x4 -> x0, other arithmetic: 4.35 us -> none  [the longest x1 1.75 us: device_step(): (dy_f32 + inv_rms * (d_norm - normed * jnp.mean(d_norm * normed, axis=-1,...]
    unnamed x32 -> x14, local copies, waits for them, and re-layouts: 9.37 us -> 13.6 us
  transfers between devices with their start and end apart: 1 -> 0, of which waited for: 1 -> 0; matrix products, arithmetic and copies ran while one was open for 2% -> 0% of each run, Pallas kernels for 0% -> 0%
where the time goes in v2:
time: 155 us
  Pallas kernels  138 us (89%)
  local copies, waits for them, and re-layouts  16.2 us (10%)
    pallas_call x1, Pallas kernels, moe(): pl.pallas_call(moe_kernel, name='moe', out_shape=out_shape, in_specs=[vme...  138 us
    unnamed x14, local copies, waits for them, and re-layouts  13.6 us

profile of v2, /device:TPU:97, one launch (start us, length us, event | category | flops | bytes accessed | tf_op | source)
XLA Modules:
  0.0 154.7 jit_solution(15604300386921226076)
XLA Ops:
  0.6 1.3 broadcast_in_dim.6.gain_ref
  1.9 1.3 broadcast_in_dim.7.bias_ref
  3.2 137.9 %moe.1 = (bf16[128,1024]{1,0:T(8,128)(2,1)}, bf16[128,1024]{1,0:T(8,128)(2,1)}, f32[1,1024]{1,0:T(1,128)}, f32[32,1024]{1,0:T(8,128)}, f32[1,1024]{1,0:T(1,128)}...) custom-call(bf16[128,1024]{1,0:T(8,128)(2,1)} %x_ref.1, bf16[128,1024]{1,0:T(8,128)(2,1)} %dy_ref.1, ...), custom_call_target="tpu_custom_call" | custom-call | tf_op jit(solution)/shard_map/moe/pallas_call | solution.py:408
  141.1 1.7 %copy.25 = bf16[128,1024]{1,0:T(8,128)(2,1)} copy(bf16[128,1024]{1,0:T(8,128)(2,1)} %get-tuple-element.32) | data formatting | bytes 524288
  142.8 1.7 %copy.26 = bf16[128,1024]{1,0:T(8,128)(2,1)} copy(bf16[128,1024]{1,0:T(8,128)(2,1)} %get-tuple-element.33) | data formatting | bytes 524288
  144.4 1.3 copy.27
  145.7 1.6 %copy.28 = f32[1024,32]{0,1:T(8,128)} copy(f32[1024,32]{0,1:T(8,128)} %bitcast.5) | data formatting | bytes 262144
  147.3 0.0 copy-start.1
  147.3 3.2 %copy.29 = f32[4,1024,128]{2,1,0:T(8,128)} copy(f32[4,1024,128]{2,1,0:T(8,128)} %get-tuple-element.36) | data formatting | bytes 4194304
  150.5 0.0 copy-done.1
  150.5 0.0 copy-start
  150.5 1.3 copy.30
  151.8 1.0 copy-done
  152.8 0.0 copy-start.2
  152.8 1.3 copy.31
  154.2 0.0 copy-done.2
  154.2 0.6 copy.32
Async XLA Ops:
  147.3 3.2 %copy-start.1 = (f32[4,1024,128]{2,1,0:T(8,128)S(1)}, f32[4,1024,128]{2,1,0:T(8,128)}, u32[]{:S(2)}) copy-start(f32[4,1024,128]{2,1,0:T(8,128)} %get-tuple-element.37) | copy-start | bytes 6291460
  150.5 2.3 %copy-start = (f32[4,128,1024]{2,1,0:T(8,128)S(1)}, f32[4,128,1024]{2,1,0:T(8,128)}, u32[]{:S(2)}) copy-start(f32[4,128,1024]{2,1,0:T(8,128)} %get-tuple-element.38) | copy-start | bytes 6291460
  152.8 1.3 copy-start.2

commit v3 on v2

--- a/solution.py
+++ b/solution.py
@@ -9,11 +9,11 @@
 MESH = pl.DeviceIdType.MESH
 F32 = jnp.float32
 BF16 = jnp.bfloat16
-ORDER = ((0, 0), (0, 1), (0, 3), (0, 2), (1, 0), (1, 1), (1, 3), (3, 1), (3, 3), (1, 2), (2, 1), (2, 3), (3, 2), (2, 2), (2, 0), (3, 0))
-ARRIVALS = {1: ((0, 1), (0, 3), (1, 0), (3, 0)), 2: ((2, 0), (0, 2)), 4: ((1, 1), (1, 3)), 6: ((3, 1), (3, 3)),
-            8: ((1, 2),), 9: ((2, 1), (2, 3)), 11: ((3, 2),), 12: ((2, 2),)}
-FIRST_AT = {4: 0, 10: 1, 13: 3, 14: 2}
-SECOND_AT = {6: 0, 12: 1, 15: 3}
+ORDER = ((0, 0), (0, 1), (0, 3), (0, 2), (1, 0), (1, 1), (1, 3), (2, 1), (2, 3), (3, 1), (1, 2), (2, 2), (3, 3), (3, 2), (2, 0), (3, 0))
+ARRIVALS = {1: ((0, 1), (0, 3), (1, 0), (3, 0)), 2: ((2, 0), (0, 2)), 4: ((1, 1), (1, 3)), 6: ((2, 1), (2, 3)),
+            8: ((3, 1), (3, 3)), 9: ((1, 2),), 10: ((2, 2),), 11: ((3, 2),)}
+FIRST_AT = {8: 0, 11: 1, 12: 2, 14: 3}
+SECOND_AT = {10: 0, 13: 1, 14: 2}
 SLOT = {place: k for k, place in enumerate(ORDER)}
 N_SLOT = len(ORDER)
 N_SEND = 67
@@ -79,7 +79,7 @@
             chosen = jnp.logical_or(chosen, expert == idx_ref[j:j + 1, :])
         return chosen
 
-    gain = gain_ref[...].astype(F32)
+    gain = gain_ref[...].astype(F32).reshape(1, d_model)
     hidden = (normalised()[2] * gain).astype(BF16)
     x_own[0, 0] = hidden
     x_own[0, 1] = dy_ref[...]
@@ -91,7 +91,7 @@
     def remote(src, dst, send, recv, dev):
         return pltpu.make_async_remote_copy(src_ref=src, dst_ref=dst, send_sem=send, recv_sem=recv, device_id=dev, device_id_type=MESH)
 
-    sends = {k: [] for k in range(N_SLOT)}
+    sends = {k: [] for k in (*range(N_SLOT), "late")}
     count = [0]
 
     def plan(k, src, dst, recv, dev):
@@ -99,9 +99,10 @@
         count[0] += 1
         sends[k].append(lambda: remote(src, dst, ag_send.at[n], recv, dev))
 
-    def plan_block(k, to, dev):
-        plan(k, x_own.at[k], x_own.at[to], ag_recv.at[to, 0], dev)
-        plan(k, g_own.at[k], g_own.at[to], ag_grecv.at[to], dev)
+    def plan_block(k, to, dev, after=None):
+        after = k if after is None else after
+        plan(after, x_own.at[k], x_own.at[to], ag_recv.at[to, 0], dev)
+        plan(after, g_own.at[k], g_own.at[to], ag_grecv.at[to], dev)
 
     plan_block(0, SLOT[(3, 0)], f_up)
     plan_block(0, SLOT[(1, 0)], f_dn)
@@ -114,8 +115,9 @@
             to = SLOT[(2, 0)]
             plan(k, x_own.at[k, 1], x_own.at[to, 1], ag_recv.at[to, 1], f_dn)
         if ds == 0:
-            plan_block(k, SLOT[(df, 3)], s_up)
-            plan_block(k, SLOT[(df, 1)], s_dn)
+            after = "late" if (df, ds) == (3, 0) else k
+            plan_block(k, SLOT[(df, 3)], s_up, after)
+            plan_block(k, SLOT[(df, 1)], s_dn, after)
         if ds == 3:
             to = SLOT[(df, 2)]
             plan(k, x_own.at[k, 0], x_own.at[to, 0], ag_recv.at[to, 0], s_up)
@@ -135,7 +137,7 @@
             else:
                 remote(x_own.at[k], x_own.at[k], ag_send.at[0], ag_recv.at[k, 0], sib).wait_recv()
             remote(g_own.at[k], g_own.at[k], ag_send.at[0], ag_grecv.at[k], sib).wait_recv()
-        for make in sends[k]:
+        for make in sends[k] + (sends["late"] if ORDER[k] == (2, 0) else []):
             make().start()
 
     def to_sibling(k):
@@ -261,7 +263,7 @@
     dbias_ref[...] = jnp.sum(acc_b[...], axis=0, keepdims=True)
     for j in range(N_SLOT - LAG, N_SLOT):
         add_sibling(j)
-    send_second(2)
+    send_second(3)
 
     k2, k1, k3 = SLOT[(2, 0)], SLOT[(1, 0)], SLOT[(3, 0)]
 
@@ -277,24 +279,33 @@
     f_first = (remote(pg_own.at[k2], r3g, f1_send.at[2], f1_recv.at[2], f_up),
                remote(part.at[k2, 0], r3.at[0], f1_send.at[0], f1_recv.at[0], f_up),
                remote(part.at[k2, 1], r3.at[1], f1_send.at[1], f1_recv.at[1], f_dn))
-    f_second = (remote(pg_own.at[k1], r4g.at[0], f2_send.at[1], f2_recv.at[1], f_up),
-                remote(pg_own.at[k3], r4g.at[1], f2_send.at[3], f2_recv.at[3], f_dn),
-                remote(part.at[k1], r4.at[0], f2_send.at[0], f2_recv.at[0], f_up),
-                remote(part.at[k3], r4.at[1], f2_send.at[2], f2_recv.at[2], f_dn))
-    for df, k in ((1, k1), (3, k3), (0, 0), (2, k2)):
+    f_second = (remote(pg_own.at[k1], r4g.at[0], f2_send.at[0], f2_recv.at[0], f_up),
+                remote(pg_own.at[k3], r4g.at[1], f2_send.at[1], f2_recv.at[1], f_dn),
+                remote(part.at[k1, 1], r4.at[0, 1], f2_send.at[2], f2_recv.at[2], f_up),
+                remote(part.at[k3, 1], r4.at[1, 1], f2_send.at[3], f2_recv.at[3], f_dn),
+                remote(part.at[k1, 0], r4.at[0, 0], f2_send.at[4], f2_recv.at[4], f_up),
+                remote(part.at[k3, 0], r4.at[1, 0], f2_send.at[5], f2_recv.at[5], f_dn))
+    for df, k in ((2, k2), (1, k1), (3, k3)):
         wait_second(df)
-        if df:
-            part[k, 0] = total(k, df, 0).astype(BF16)
-            part[k, 1] = total(k, df, 1).astype(BF16)
-    for c in f_first:
-        c.start()
-    for c in f_first:
-        c.wait_recv()
-    pg_own[k1] = pg_own[k1] + r3g[...]
-    add_into(k1, 0, r3.at[0])
+        part[k, 0] = total(k, df, 0).astype(BF16)
+        part[k, 1] = total(k, df, 1).astype(BF16)
+        if df == 2:
+            for c in f_first:
+                c.start()
+        if df == 1:
+            f_first[0].wait_recv()
+            pg_own[k1] = pg_own[k1] + r3g[...]
+            f_second[0].start()
+            f_second[2].start()
+            f_first[1].wait_recv()
+            add_into(k1, 0, r3.at[0])
+            f_second[4].start()
+    f_second[1].start()
+    f_first[2].wait_recv()
     add_into(k3, 1, r3.at[1])
-    for c in f_second:
-        c.start()
+    f_second[3].start()
+    f_second[5].start()
+    wait_second(0)
 
     for c in f_second[:2]:
         c.wait_recv()
@@ -303,65 +314,74 @@
     d_logits = gates * (d_gates - jnp.sum(gates * d_gates, axis=0, keepdims=True))
     dl_buf[0, 0] = d_logits
     dh_router = lax.dot_general(d_logits, router_ref[...].astype(F32), (((0,), (0,)), ((), ())), precision=lax.Precision.HIGHEST, preferred_element_type=F32)
-    f_dl = [remote(dl_buf.at[0, 0], dl_buf.at[0, to], e_send.at[i], e_recv.at[i], dev) for i, (to, dev) in enumerate(((3, f_up), (1, f_dn), (2, f_op)))]
-    s_dl = [remote(dl_buf.at[0], dl_buf.at[to], e_send.at[3 + i], e_recv.at[3 + i], dev) for i, (to, dev) in enumerate(((3, s_up), (1, s_dn), (2, s_op)))]
+    s_dl = [remote(dl_buf.at[0, 0], dl_buf.at[0, to], e_send.at[i], e_recv.at[i], dev) for i, (to, dev) in enumerate(((3, s_up), (1, s_dn), (2, s_op)))]
+    f_dl = [remote(dl_buf.at[0], dl_buf.at[to], e_send.at[3 + i], e_recv.at[3 + i], dev) for i, (to, dev) in enumerate(((3, f_up), (1, f_dn), (2, f_op)))]
+    for c in s_dl:
+        c.start()
+
+    for c in f_second[2:4]:
+        c.wait_recv()
+    x, inv_rms, normed = normalised()
+    dh_total = total(0, 0, 1) + r4[0, 1].astype(F32) + r4[1, 1].astype(F32) + dh_router
+    gn_buf[0] = jnp.sum(dh_total * normed, axis=0, keepdims=True)
+
+    def exchange(base, group, first_sem):
+        return [remote(gn_buf.at[base], gn_buf.at[base + 1 + i], e_send.at[first_sem + i], e_recv.at[first_sem + i], dev) for i, dev in enumerate(group)]
+
+    def gathered(base, copies):
+        for c in copies:
+            c.wait_recv()
+        summed = gn_buf[base]
+        for i in range(len(copies)):
+            summed = summed + gn_buf[base + 1 + i]
+        return summed
+
+    gn_sib = exchange(0, (sib,), 7)
+    for c in gn_sib:
+        c.start()
+    for c in s_dl:
+        c.wait_recv()
     for c in f_dl:
         c.start()
+    d_norm = dh_total * gain
+    dx_ref[...] = (dy_ref[...].astype(F32) + inv_rms * (d_norm - normed * jnp.mean(d_norm * normed, axis=-1, keepdims=True))).astype(BF16)
+    gn_buf[2] = gathered(0, gn_sib)
+    gn_s = exchange(2, (s_up, s_dn, s_op), 8)
+    for c in gn_s:
+        c.start()
+    d_router = jnp.zeros((n_exp, d_model), F32)
     for c in f_dl:
         c.wait_recv()
-    for c in s_dl:
-        c.start()
-    for c in s_dl:
-        c.wait_recv()
-    d_router = jnp.zeros((n_exp, d_model), F32)
     for k, (df, ds) in enumerate(ORDER):
-        dl = dl_buf[ds, df]
+        dl = dl_buf[df, ds]
         dl_hi = dl.astype(BF16)
         dl_lo = (dl - dl_hi.astype(F32)).astype(BF16)
         prods = jnp.dot(jnp.concatenate([dl_hi, dl_lo], axis=0), x_own[k, 0], preferred_element_type=F32)
         d_router = d_router + (prods[:n_exp] + prods[n_exp:])
+        if k == 3:
+            gn_buf[6] = gathered(2, gn_s)
+            gn_f = exchange(6, (f_up, f_dn, f_op), 11)
+            for c in gn_f:
+                c.start()
     dr_buf[0] = d_router
-
-    for c in f_second[2:]:
-        c.wait_recv()
     sib_dr = remote(dr_buf.at[0], dr_buf.at[1], e_send.at[6], e_recv.at[6], sib)
     sib_dr.start()
-    x, inv_rms, normed = normalised()
-    dh_total = total(0, 0, 1) + r4[0, 1].astype(F32) + r4[1, 1].astype(F32) + dh_router
-    gn_buf[0] = jnp.sum(dh_total * normed, axis=0, keepdims=True)
-    d_norm = dh_total * gain
-    dx_ref[...] = (dy_ref[...].astype(F32) + inv_rms * (d_norm - normed * jnp.mean(d_norm * normed, axis=-1, keepdims=True))).astype(BF16)
-    exchanges = [sib_dr]
-    n_sem = 7
-    for group in ((f_up, f_dn, f_op), (s_up, s_dn, s_op), (sib,)):
-        base = n_sem - 7
-        copies = [remote(gn_buf.at[base], gn_buf.at[base + 1 + i], e_send.at[n_sem + i], e_recv.at[n_sem + i], dev) for i, dev in enumerate(group)]
-        for c in copies:
-            c.start()
-        if base == 0:
-            y_moe = total(0, 0, 0) + r4[0, 0].astype(F32) + r4[1, 0].astype(F32)
-            y_ref[...] = (x + (y_moe + bias_ref[...].astype(F32))).astype(BF16)
-        for c in copies:
-            c.wait_recv()
-        summed = gn_buf[base]
-        for i in range(len(group)):
-            summed = summed + gn_buf[base + 1 + i]
-        exchanges += copies
-        n_sem += len(group) + 1
-        if len(group) > 1:
-            gn_buf[n_sem - 7] = summed
-        else:
-            dgain_ref[...] = summed
+    for c in f_second[4:]:
+        c.wait_recv()
+    y_moe = total(0, 0, 0) + r4[0, 0].astype(F32) + r4[1, 0].astype(F32)
+    y_ref[...] = (x + (y_moe + bias_ref[...].astype(F32).reshape(1, d_model))).astype(BF16)
+    dgain_ref[...] = gathered(6, gn_f)
     sib_dr.wait_recv()
     drouter_ref[...] = dr_buf[0] + dr_buf[1]
 
-    for c in f_dl + s_dl + exchanges:
+    for c in f_dl + s_dl + gn_sib + gn_s + gn_f + [sib_dr]:
         c.wait_send()
     for c in stores:
         c.wait()
+    for made in sends.values():
+        for make in made:
+            make().wait_send()
     for k in range(N_SLOT):
-        for make in sends[k]:
-            make().wait_send()
         for c in to_sibling(k):
             c.wait_send()
     for df in range(4):
@@ -398,7 +418,7 @@
         pltpu.VMEM((d_model, 2 * loc), F32), pltpu.VMEM((loc, d_model), F32), pltpu.VMEM((8, d_model), F32),
         dma((3 * n_loc,)), dma((N_SEND,)), dma((N_SLOT, 2)), dma((N_SLOT,)), dma((N_SLOT, 2)),
         dma((N_SLOT, 2)), dma((N_SLOT, 2)), dma((4, 3)), dma((4, 3)), dma((4, 2, 2)), dma((4, 2, 2)),
-        dma((3,)), dma((3,)), dma((4,)), dma((4,)), dma((17,)), dma((17,)),
+        dma((3,)), dma((3,)), dma((6,)), dma((6,)), dma((14,)), dma((14,)),
     ]
     out_shape = (
         jax.ShapeDtypeStruct((n_tok, d_model), BF16), jax.ShapeDtypeStruct((n_tok, d_model), BF16),
@@ -413,6 +433,36 @@
     )(x, dy, idx_t, gain, bias, router_t, w_gate, w_up, w_down)
 
 
+def write_out(*refs):
+    n = len(refs) // 3
+    sources, results, rooms, sems = refs[:n], refs[n:2 * n], refs[2 * n:3 * n], refs[3 * n]
+    pieces = []
+    for i in range(n):
+        for j in range(sources[i].shape[0] if len(sources[i].shape) == 3 else 1):
+            at = (lambda r, j=j: r.at[j]) if len(sources[i].shape) == 3 else (lambda r: r)
+            m = len(pieces)
+            pieces.append((pltpu.make_async_copy(at(sources[i]), at(rooms[i]), sems.at[m, 0]),
+                           pltpu.make_async_copy(at(rooms[i]), at(results[i]), sems.at[m, 1])))
+    for load, _ in pieces:
+        load.start()
+    for load, store in pieces:
+        load.wait()
+        store.start()
+    for _, store in pieces:
+        store.wait()
+
+
+def finish(*arrays):
+    hbm = pl.BlockSpec(memory_space=pl.ANY)
+    n_pieces = sum(a.shape[0] if a.ndim == 3 else 1 for a in arrays)
+    return pl.pallas_call(
+        write_out, name="finish", out_shape=tuple(jax.ShapeDtypeStruct(a.shape, a.dtype) for a in arrays),
+        in_specs=[hbm] * len(arrays), out_specs=(hbm,) * len(arrays),
+        scratch_shapes=[pltpu.VMEM(a.shape, a.dtype) for a in arrays] + [pltpu.SemaphoreType.DMA((n_pieces, 2))],
+        compiler_params=pltpu.CompilerParams(vmem_limit_bytes=32 << 20),
+    )(*arrays)
+
+
 def solution(mesh):
     tok_spec = P(("dp", "ep", "tp"), None)
     wide_spec = P("ep", None, "tp")
@@ -422,7 +472,8 @@
 
     def device_step(x_in, norm_gain, w_router, expert_idx, w_gate, w_up, w_down, out_bias, dy_out):
         y_out, dx_in, d_gain, d_router_t, d_bias, d_gate, d_up, d_down = moe(
-            x_in, dy_out, expert_idx.T, norm_gain[None, :], out_bias[None, :], w_router.T, w_gate, w_up, w_down)
+            x_in, dy_out, expert_idx.T, norm_gain, out_bias, w_router.T, w_gate, w_up, w_down)
+        y_out, dx_in, d_gate, d_up, d_down = finish(y_out, dx_in, d_gate, d_up, d_down)
         return y_out, dx_in, d_gain[0], d_router_t.T, d_gate, d_up, d_down, d_bias[0]
 
     return jax.shard_map(device_step, mesh=mesh, in_specs=(tok_spec, P(None), P(None, None), tok_spec, wide_spec, wide_spec, down_spec, P(None), tok_spec), out_specs=(tok_spec, tok_spec, P("dp"), P("dp", None), grad_wide, grad_wide, grad_down, P("dp")), check_vma=False)

time: 155 us -> 138 us (0.89)
  Pallas kernels: 138 us -> 128 us
  local copies, waits for them, and re-layouts: 16.2 us -> 8.52 us
    pallas_call x1, Pallas kernels: 138 us -> 125 us  [moe(): pl.pallas_call(moe_kernel, name='moe', out_shape=out_shape, in_specs=[vme...]
    unnamed x14 -> x19, local copies, waits for them, and re-layouts: 13.6 us -> 8.52 us
    pallas_call x0 -> x1, Pallas kernels: none -> 3.51 us  [finish(): pl.pallas_call(write_out, name='finish', out_shape=tuple((jax.ShapeDtypeS...]
    broadcast_in_dim x2 -> x0, local copies, waits for them, and re-layouts: 2.56 us -> none  [the longest x1 1.28 us: device_step(): norm_gain[None, :]]
where the time goes in v3:
time: 138 us
  Pallas kernels  128 us (93%)
  local copies, waits for them, and re-layouts  8.52 us (6%)
    pallas_call x1, Pallas kernels, moe(): pl.pallas_call(moe_kernel, name='moe', out_shape=out_shape, in_specs=[vme...  125 us
    unnamed x19, local copies, waits for them, and re-layouts  8.52 us
    pallas_call x1, Pallas kernels, finish(): pl.pallas_call(write_out, name='finish', out_shape=tuple((jax.ShapeDtypeS...  3.51 us

profile of v3, /device:TPU:97, one launch (start us, length us, event | category | flops | bytes accessed | tf_op | source)
XLA Modules:
  0.0 137.6 jit_solution(7876596485794275317)
XLA Ops:
  0.6 124.9 %moe.1 = (bf16[128,1024]{1,0:T(8,128)(2,1)}, bf16[128,1024]{1,0:T(8,128)(2,1)}, f32[1,1024]{1,0:T(1,128)}, f32[32,1024]{1,0:T(8,128)}, f32[1,1024]{1,0:T(1,128)}...) custom-call(bf16[128,1024]{1,0:T(8,128)(2,1)} %x_ref.1, bf16[128,1024]{1,0:T(8,128)(2,1)} %dy_ref.1, ...), custom_call_target="tpu_custom_call" | custom-call | tf_op jit(solution)/shard_map/moe/pallas_call | solution.py:428
  125.5 0.0 copy-start
  125.5 1.6 %copy-done = f32[4,1024,128]{2,1,0:T(8,128)S(1)} copy-done((f32[4,1024,128]{2,1,0:T(8,128)S(1)}, f32[4,1024,128]{2,1,0:T(8,128)}, u32[]{:S(2)}) %copy-start) | copy-done | bytes 2097176
  127.1 0.0 copy-start.1
  127.1 1.6 %copy-done.1 = f32[4,1024,128]{2,1,0:T(8,128)S(1)} copy-done((f32[4,1024,128]{2,1,0:T(8,128)S(1)}, f32[4,1024,128]{2,1,0:T(8,128)}, u32[]{:S(2)}) %copy-start.1) | copy-done | bytes 2097176
  128.7 0.0 copy-start.2
  128.7 1.6 %copy-done.2 = f32[4,128,1024]{2,1,0:T(8,128)S(1)} copy-done((f32[4,128,1024]{2,1,0:T(8,128)S(1)}, f32[4,128,1024]{2,1,0:T(8,128)}, u32[]{:S(2)}) %copy-start.2) | copy-done | bytes 2097176
  130.3 0.0 copy-start.3
  130.3 0.9 copy-done.3
  131.3 0.0 copy-start.4
  131.3 0.9 copy-done.4
  132.2 0.0 copy-start.7
  132.2 0.0 copy-start.5
  132.2 0.0 copy-start.6
  132.2 3.5 %finish.1 = (bf16[128,1024]{1,0:T(8,128)(2,1)}, bf16[128,1024]{1,0:T(8,128)(2,1)}, f32[4,1024,128]{2,1,0:T(8,128)}, f32[4,1024,128]{2,1,0:T(8,128)}, f32[4,128,1024]{2,1,0:T(8,128)}) custom-call(bf16[128,1024]{1,0:T(8,128)(2,1)S(1)} %copy-done.3, bf16[128,1024]{1,0:T(8,128)(2,1)S(1)} %copy-done.4, f32[4,1024,128]{2,1,0:T(8,128)S(1)} %copy-done, ...), custom_call_target="tpu_custom_call" | custom-call | tf_op jit(solution)/shard_map/finish/pallas_call | solution.py:458
  135.7 0.0 copy-done.7
  135.7 0.6 copy.20
  136.3 0.0 copy-done.5
  136.3 0.7 copy.21
  137.0 0.0 copy-done.6
  137.0 0.6 copy.22
Async XLA Ops:
  125.5 1.6 %copy-start = (f32[4,1024,128]{2,1,0:T(8,128)S(1)}, f32[4,1024,128]{2,1,0:T(8,128)}, u32[]{:S(2)}) copy-start(f32[4,1024,128]{2,1,0:T(8,128)} %get-tuple-element.23.refs_2_) | copy-start | bytes 6291460
  127.1 1.6 %copy-start.1 = (f32[4,1024,128]{2,1,0:T(8,128)S(1)}, f32[4,1024,128]{2,1,0:T(8,128)}, u32[]{:S(2)}) copy-start(f32[4,1024,128]{2,1,0:T(8,128)} %get-tuple-element.24.refs_3_) | copy-start | bytes 6291460
  128.7 1.6 %copy-start.2 = (f32[4,128,1024]{2,1,0:T(8,128)S(1)}, f32[4,128,1024]{2,1,0:T(8,128)}, u32[]{:S(2)}) copy-start(f32[4,128,1024]{2,1,0:T(8,128)} %get-tuple-element.25.refs_4_) | copy-start | bytes 6291460
  130.3 0.9 copy-start.3
  131.3 0.9 copy-start.4
  132.2 3.5 %copy-start.7 = (f32[1,1024]{1,0:T(1,128)S(1)}, f32[1,1024]{1,0:T(1,128)}, u32[]{:S(2)}) copy-start(f32[1,1024]{1,0:T(1,128)} %get-tuple-element.28) | copy-start | bytes 12292
  132.2 4.1 %copy-start.5 = (f32[32,1024]{1,0:T(8,128)S(1)}, f32[32,1024]{1,0:T(8,128)}, u32[]{:S(2)}) copy-start(f32[32,1024]{1,0:T(8,128)} %get-tuple-element.29) | copy-start | bytes 393220
  132.2 4.8 %copy-start.6 = (f32[1,1024]{1,0:T(1,128)S(1)}, f32[1,1024]{1,0:T(1,128)}, u32[]{:S(2)}) copy-start(f32[1,1024]{1,0:T(1,128)} %get-tuple-element.33) | copy-start | bytes 12292

commit v4 on v3

--- a/solution.py
+++ b/solution.py
@@ -10,7 +10,7 @@
 F32 = jnp.float32
 BF16 = jnp.bfloat16
 ORDER = ((0, 0), (0, 1), (0, 3), (0, 2), (1, 0), (1, 1), (1, 3), (2, 1), (2, 3), (3, 1), (1, 2), (2, 2), (3, 3), (3, 2), (2, 0), (3, 0))
-ARRIVALS = {1: ((0, 1), (0, 3), (1, 0), (3, 0)), 2: ((2, 0), (0, 2)), 4: ((1, 1), (1, 3)), 6: ((2, 1), (2, 3)),
+ARRIVALS = {1: ((0, 1), (0, 3)), 2: ((1, 0), (3, 0), (0, 2)), 3: ((2, 0),), 4: ((1, 1), (1, 3)), 6: ((2, 1), (2, 3)),
             8: ((3, 1), (3, 3)), 9: ((1, 2),), 10: ((2, 2),), 11: ((3, 2),)}
 FIRST_AT = {8: 0, 11: 1, 12: 2, 14: 3}
 SECOND_AT = {10: 0, 13: 1, 14: 2}
@@ -27,7 +27,7 @@
 def moe_kernel(x_ref, dy_ref, idx_ref, gain_ref, bias_ref, router_ref, wg_ref, wu_ref, wd_ref,
                y_ref, dx_ref, dgain_ref, drouter_ref, dbias_ref, dwg_ref, dwu_ref, dwd_ref,
                x_own, x_sib, part, g_own, g_sib, pg_own, pg_sib, q_buf, qg_buf,
-               r1, r1g, r2, r2g, r3, r3g, r4, r4g, dl_buf, dr_buf, gn_buf, wgu, wd, acc_gu, acc_d, acc_b,
+               r1, r1g, r2, r2g, r3, r3g, r4, r4g, dl_buf, dr_buf, gn_buf, wgu, wd, acc_gu, acc_d,
                load_sem, ag_send, ag_recv, ag_grecv, sib_recv,
                rq_send, rq_recv, s1_send, s1_recv, s2_send, s2_recv, f1_send, f1_recv, f2_send, f2_recv, e_send, e_recv):
     ep = lax.axis_index("ep")
@@ -91,7 +91,7 @@
     def remote(src, dst, send, recv, dev):
         return pltpu.make_async_remote_copy(src_ref=src, dst_ref=dst, send_sem=send, recv_sem=recv, device_id=dev, device_id_type=MESH)
 
-    sends = {k: [] for k in (*range(N_SLOT), "late")}
+    sends = {k: [] for k in (*range(N_SLOT), "late", "own")}
     count = [0]
 
     def plan(k, src, dst, recv, dev):
@@ -104,8 +104,8 @@
         plan(after, x_own.at[k], x_own.at[to], ag_recv.at[to, 0], dev)
         plan(after, g_own.at[k], g_own.at[to], ag_grecv.at[to], dev)
 
-    plan_block(0, SLOT[(3, 0)], f_up)
-    plan_block(0, SLOT[(1, 0)], f_dn)
+    plan_block(0, SLOT[(3, 0)], f_up, "own")
+    plan_block(0, SLOT[(1, 0)], f_dn, "own")
     for k, (df, ds) in enumerate(ORDER):
         if (df, ds) == (3, 0):
             to = SLOT[(2, 0)]
@@ -178,38 +178,42 @@
 
     row = lax.broadcasted_iota(jnp.int32, (n_exp, loc), 0)
     col = lax.broadcasted_iota(jnp.int32, (n_exp, loc), 1)
-    pick = jnp.where(row == ep * n_loc + lax.div(col, width), 1.0, 0.0).astype(F32)
+    pick = jnp.where(row == ep * n_loc + lax.div(col, width), 1.0, 0.0).astype(BF16)
+    pick3 = jnp.concatenate([pick] * 3, axis=0)
+    ones = jnp.ones((16, 2 * n_tok), BF16)
 
     def widen(g):
-        return lax.dot_general(g, pick, (((0,), (0,)), ((), ())), precision=lax.Precision.HIGHEST, preferred_element_type=F32)
+        hi = g.astype(BF16)
+        rest = g - hi.astype(F32)
+        mid = rest.astype(BF16)
+        low = (rest - mid.astype(F32)).astype(BF16)
+        return lax.dot_general(jnp.concatenate([hi, mid, low], axis=0), pick3, (((0,), (0,)), ((), ())), preferred_element_type=F32)
 
     def compute(k):
         h = jnp.concatenate([x_own[k, 0], x_sib[k, 0]], axis=0)
         dy = jnp.concatenate([x_own[k, 1], x_sib[k, 1]], axis=0)
-        gate = jnp.concatenate([widen(g_own[k]), widen(g_sib[k])], axis=0)
+        gate = widen(jnp.concatenate([g_own[k], g_sib[k]], axis=1))
         both = jnp.dot(h, wgu[...], preferred_element_type=F32)
         g_pre = both[:, :loc]
         u_pre = both[:, loc:]
         d_raw = dot_nt(dy, wd[...])
         used = gate != 0.0
-        sig = jax.nn.sigmoid(g_pre)
+        sig = 0.5 * jnp.tanh(0.5 * g_pre) + 0.5
         silu = g_pre * sig
         act = (silu * u_pre).astype(BF16).astype(F32)
         act_g = jnp.where(used, gate * act, 0.0).astype(BF16)
         prod = jnp.where(used, act * d_raw, 0.0)
         d_act = gate * d_raw
-        d_g = jnp.where(used, d_act * u_pre * sig * (1.0 + g_pre * (1.0 - sig)), 0.0).astype(BF16)
+        d_g = jnp.where(used, d_act * u_pre * (sig + silu * (1.0 - sig)), 0.0).astype(BF16)
         d_u = jnp.where(used, d_act * silu, 0.0).astype(BF16)
         d_gu = jnp.concatenate([d_g, d_u], axis=1)
         prod_hi = prod.astype(BF16)
         prod_lo = (prod - prod_hi.astype(F32)).astype(BF16)
-        pick_b = pick.astype(BF16)
-        dgate = dot_nt(pick_b, prod_hi) + dot_nt(pick_b, prod_lo)
+        dgate = dot_nt(pick, prod_hi) + dot_nt(pick, prod_lo)
         pg_own[k] = dgate[:, :n_tok]
         pg_sib[k] = dgate[:, n_tok:]
-        acc_b[...] += jnp.sum(dy.astype(F32).reshape(2 * n_tok // 8, 8, d_model), axis=0)
         acc_gu[...] += jnp.dot(h.T, d_gu, preferred_element_type=F32)
-        acc_d[...] += jnp.dot(act_g.T, dy, preferred_element_type=F32)
+        acc_d[...] += jnp.dot(jnp.concatenate([act_g.T, ones], axis=0), dy, preferred_element_type=F32)
         y = jnp.dot(act_g, wd[...], preferred_element_type=F32).astype(BF16)
         part[k, 0] = y[:n_tok]
         x_sib[k, 0] = y[n_tok:]
@@ -220,7 +224,6 @@
     arrive(0)
     acc_gu[...] = jnp.zeros_like(acc_gu)
     acc_d[...] = jnp.zeros_like(acc_d)
-    acc_b[...] = jnp.zeros_like(acc_b)
     for c in loads:
         c.wait()
 
@@ -228,6 +231,9 @@
         for j, places in ARRIVALS.items():
             @pl.when(k == j)
             def _():
+                if j == 1:
+                    for make in sends["own"]:
+                        make().start()
                 for place in places:
                     arrive(SLOT[place])
         remote(x_own.at[k], x_sib.at[k], ag_send.at[0], sib_recv.at[k, 0], sib).wait_recv()
@@ -260,7 +266,7 @@
         stores.append(pltpu.make_async_copy(acc_d.at[cols], dwd_ref.at[e], load_sem.at[len(stores)]))
     for c in stores:
         c.start()
-    dbias_ref[...] = jnp.sum(acc_b[...], axis=0, keepdims=True)
+    dbias_ref[...] = acc_d[loc:loc + 1]
     for j in range(N_SLOT - LAG, N_SLOT):
         add_sibling(j)
     send_second(3)
@@ -415,7 +421,7 @@
         pltpu.VMEM((2, *block), BF16), pltpu.VMEM((2, *small), F32),
         pltpu.VMEM((4, 4, *small), F32), pltpu.VMEM((2, n_exp, d_model), F32), pltpu.VMEM((10, 1, d_model), F32),
         pltpu.VMEM((d_model, 2 * loc), BF16), pltpu.VMEM((loc, d_model), BF16),
-        pltpu.VMEM((d_model, 2 * loc), F32), pltpu.VMEM((loc, d_model), F32), pltpu.VMEM((8, d_model), F32),
+        pltpu.VMEM((d_model, 2 * loc), F32), pltpu.VMEM((loc + 16, d_model), F32),
         dma((3 * n_loc,)), dma((N_SEND,)), dma((N_SLOT, 2)), dma((N_SLOT,)), dma((N_SLOT, 2)),
         dma((N_SLOT, 2)), dma((N_SLOT, 2)), dma((4, 3)), dma((4, 3)), dma((4, 2, 2)), dma((4, 2, 2)),
         dma((3,)), dma((3,)), dma((6,)), dma((6,)), dma((14,)), dma((14,)),
@@ -459,7 +465,7 @@
         write_out, name="finish", out_shape=tuple(jax.ShapeDtypeStruct(a.shape, a.dtype) for a in arrays),
         in_specs=[hbm] * len(arrays), out_specs=(hbm,) * len(arrays),
         scratch_shapes=[pltpu.VMEM(a.shape, a.dtype) for a in arrays] + [pltpu.SemaphoreType.DMA((n_pieces, 2))],
-        compiler_params=pltpu.CompilerParams(vmem_limit_bytes=32 << 20),
+        compiler_params=pltpu.CompilerParams(vmem_limit_bytes=67_043_328),
     )(*arrays)
 
 

time: 138 us -> 131 us (0.949)
  local copies, waits for them, and re-layouts: 8.52 us -> 4.12 us
  Pallas kernels: 128 us -> 125 us
    pallas_call x1, Pallas kernels: 125 us -> 120 us  [moe(): pl.pallas_call(moe_kernel, name='moe', out_shape=out_shape, in_specs=[vme...]
    unnamed x19 -> x3, local copies, waits for them, and re-layouts: 8.52 us -> 4.12 us
    pallas_call x1, Pallas kernels: 3.51 us -> 5.66 us  [finish(): pl.pallas_call(write_out, name='finish', out_shape=tuple((jax.ShapeDtypeS...]
where the time goes in v4:
time: 131 us; the launch traced here: 130 us
  Pallas kernels  125 us (95%)
  local copies, waits for them, and re-layouts  4.12 us (3%)
    pallas_call x1, Pallas kernels, moe(): pl.pallas_call(moe_kernel, name='moe', out_shape=out_shape, in_specs=[vme...  120 us
    pallas_call x1, Pallas kernels, finish(): pl.pallas_call(write_out, name='finish', out_shape=tuple((jax.ShapeDtypeS...  5.66 us
    unnamed x3, local copies, waits for them, and re-layouts  4.12 us

profile of v4, /device:TPU:97, one launch (start us, length us, event | category | flops | bytes accessed | tf_op | source)
XLA Modules:
  0.0 130.3 jit_solution(4096469452439315005)
XLA Ops:
  0.6 119.8 %moe.1 = (bf16[128,1024]{1,0:T(8,128)(2,1)}, bf16[128,1024]{1,0:T(8,128)(2,1)}, f32[1,1024]{1,0:T(1,128)}, f32[32,1024]{1,0:T(8,128)}, f32[1,1024]{1,0:T(1,128)}...) custom-call(bf16[128,1024]{1,0:T(8,128)(2,1)} %x_ref.1, bf16[128,1024]{1,0:T(8,128)(2,1)} %dy_ref.1, ...), custom_call_target="tpu_custom_call" | custom-call | tf_op jit(solution)/shard_map/moe/pallas_call | solution.py:434
  120.5 5.7 %finish.1 = (bf16[128,1024]{1,0:T(8,128)(2,1)}, bf16[128,1024]{1,0:T(8,128)(2,1)}, f32[4,1024,128]{2,1,0:T(8,128)}, f32[4,1024,128]{2,1,0:T(8,128)}, f32[4,128,1024]{2,1,0:T(8,128)}) custom-call(bf16[128,1024]{1,0:T(8,128)(2,1)} %get-tuple-element.21.refs_0_, bf16[128,1024]{1,0:T(8,128)(2,1)} %get-tuple-element.22.refs_1_, ...), custom_call_target="tpu_custom_call" | custom-call | tf_op jit(solution)/shard_map/finish/pallas_call | solution.py:464
  126.1 1.3 copy.20
  127.4 1.6 %copy.21 = f32[1024,32]{0,1:T(8,128)} copy(f32[1024,32]{0,1:T(8,128)} %bitcast.5) | data formatting | bytes 262144
  129.0 1.3 copy.22

commit v5 on v4

--- a/solution.py
+++ b/solution.py
@@ -258,6 +258,8 @@
 
     lax.fori_loop(0, N_SLOT, step, 0)
 
+    send_second(3)
+
     stores = []
     for e in range(n_loc):
         cols = pl.ds(e * width, width)
@@ -269,7 +271,6 @@
     dbias_ref[...] = acc_d[loc:loc + 1]
     for j in range(N_SLOT - LAG, N_SLOT):
         add_sibling(j)
-    send_second(3)
 
     k2, k1, k3 = SLOT[(2, 0)], SLOT[(1, 0)], SLOT[(3, 0)]
 
@@ -305,29 +306,34 @@
             f_second[2].start()
             f_first[1].wait_recv()
             add_into(k1, 0, r3.at[0])
-            f_second[4].start()
     f_second[1].start()
     f_first[2].wait_recv()
     add_into(k3, 1, r3.at[1])
     f_second[3].start()
-    f_second[5].start()
+
+    gates = g_own[0]
+    chosen = chosen_mask()
+    x, inv_rms, normed = normalised()
     wait_second(0)
-
     for c in f_second[:2]:
         c.wait_recv()
-    gates = g_own[0]
-    d_gates = jnp.where(chosen_mask(), pg_own[0] + r4g[0] + r4g[1], 0.0)
+    d_gates = jnp.where(chosen, pg_own[0] + r4g[0] + r4g[1], 0.0)
     d_logits = gates * (d_gates - jnp.sum(gates * d_gates, axis=0, keepdims=True))
     dl_buf[0, 0] = d_logits
-    dh_router = lax.dot_general(d_logits, router_ref[...].astype(F32), (((0,), (0,)), ((), ())), precision=lax.Precision.HIGHEST, preferred_element_type=F32)
     s_dl = [remote(dl_buf.at[0, 0], dl_buf.at[0, to], e_send.at[i], e_recv.at[i], dev) for i, (to, dev) in enumerate(((3, s_up), (1, s_dn), (2, s_op)))]
     f_dl = [remote(dl_buf.at[0], dl_buf.at[to], e_send.at[3 + i], e_recv.at[3 + i], dev) for i, (to, dev) in enumerate(((3, f_up), (1, f_dn), (2, f_op)))]
     for c in s_dl:
         c.start()
+    dh_router = lax.dot_general(d_logits, router_ref[...].astype(F32), (((0,), (0,)), ((), ())), precision=lax.Precision.HIGHEST, preferred_element_type=F32)
+    for c in s_dl:
+        c.wait_recv()
+    for c in f_dl:
+        c.start()
+    f_second[4].start()
+    f_second[5].start()
 
     for c in f_second[2:4]:
         c.wait_recv()
-    x, inv_rms, normed = normalised()
     dh_total = total(0, 0, 1) + r4[0, 1].astype(F32) + r4[1, 1].astype(F32) + dh_router
     gn_buf[0] = jnp.sum(dh_total * normed, axis=0, keepdims=True)
 
@@ -344,10 +350,6 @@
 
     gn_sib = exchange(0, (sib,), 7)
     for c in gn_sib:
-        c.start()
-    for c in s_dl:
-        c.wait_recv()
-    for c in f_dl:
         c.start()
     d_norm = dh_total * gain
     dx_ref[...] = (dy_ref[...].astype(F32) + inv_rms * (d_norm - normed * jnp.mean(d_norm * normed, axis=-1, keepdims=True))).astype(BF16)
@@ -479,7 +481,7 @@
     def device_step(x_in, norm_gain, w_router, expert_idx, w_gate, w_up, w_down, out_bias, dy_out):
         y_out, dx_in, d_gain, d_router_t, d_bias, d_gate, d_up, d_down = moe(
             x_in, dy_out, expert_idx.T, norm_gain, out_bias, w_router.T, w_gate, w_up, w_down)
-        y_out, dx_in, d_gate, d_up, d_down = finish(y_out, dx_in, d_gate, d_up, d_down)
+        y_out, dx_in, d_gain, d_router_t, d_gate, d_up, d_down, d_bias = finish(y_out, dx_in, d_gain, d_router_t, d_gate, d_up, d_down, d_bias)
         return y_out, dx_in, d_gain[0], d_router_t.T, d_gate, d_up, d_down, d_bias[0]
 
     return jax.shard_map(device_step, mesh=mesh, in_specs=(tok_spec, P(None), P(None, None), tok_spec, wide_spec, wide_spec, down_spec, P(None), tok_spec), out_specs=(tok_spec, tok_spec, P("dp"), P("dp", None), grad_wide, grad_wide, grad_down, P("dp")), check_vma=False)

time: 131 us -> 127 us (0.969)
  local copies, waits for them, and re-layouts: 4.12 us -> 0 us
  Pallas kernels: 125 us -> 127 us
    unnamed x3 -> x0, local copies, waits for them, and re-layouts: 4.12 us -> none
where the time goes in v5:
time: 127 us
  Pallas kernels  127 us (100%)
    pallas_call x1, Pallas kernels, moe(): pl.pallas_call(moe_kernel, name='moe', out_shape=out_shape, in_specs=[vme...  121 us
    pallas_call x1, Pallas kernels, finish(): pl.pallas_call(write_out, name='finish', out_shape=tuple((jax.ShapeDtypeS...  5.69 us

profile of v5, /device:TPU:97, one launch (start us, length us, event | category | flops | bytes accessed | tf_op | source)
XLA Modules:
  0.0 127.2 jit_solution(3515795702359118874)
XLA Ops:
  0.6 120.8 %moe.1 = (bf16[128,1024]{1,0:T(8,128)(2,1)}, bf16[128,1024]{1,0:T(8,128)(2,1)}, f32[1,1024]{1,0:T(1,128)}, f32[32,1024]{1,0:T(8,128)}, f32[1,1024]{1,0:T(1,128)}...) custom-call(bf16[128,1024]{1,0:T(8,128)(2,1)} %x_ref.1, bf16[128,1024]{1,0:T(8,128)(2,1)} %dy_ref.1, ...), custom_call_target="tpu_custom_call" | custom-call | tf_op jit(solution)/shard_map/moe/pallas_call | solution.py:436
  121.5 5.7 %finish.1 = (bf16[128,1024]{1,0:T(8,128)(2,1)}, bf16[128,1024]{1,0:T(8,128)(2,1)}, f32[1,1024]{1,0:T(1,128)}, f32[32,1024]{1,0:T(8,128)}, f32[4,1024,128]{2,1,0:...) custom-call(bf16[128,1024]{1,0:T(8,128)(2,1)} %get-tuple-element.24.refs_0_, ...), custom_call_target="tpu_custom_call" | custom-call | tf_op jit(solution)/shard_map/finish/pallas_call | solution.py:466

commit v6 on v5

--- a/solution.py
+++ b/solution.py
@@ -9,11 +9,11 @@
 MESH = pl.DeviceIdType.MESH
 F32 = jnp.float32
 BF16 = jnp.bfloat16
-ORDER = ((0, 0), (0, 1), (0, 3), (0, 2), (1, 0), (1, 1), (1, 3), (2, 1), (2, 3), (3, 1), (1, 2), (2, 2), (3, 3), (3, 2), (2, 0), (3, 0))
+ORDER = ((0, 0), (0, 1), (0, 3), (0, 2), (1, 0), (1, 1), (1, 3), (2, 1), (2, 3), (1, 2), (2, 2), (3, 1), (3, 3), (3, 2), (2, 0), (3, 0))
 ARRIVALS = {1: ((0, 1), (0, 3)), 2: ((1, 0), (3, 0), (0, 2)), 3: ((2, 0),), 4: ((1, 1), (1, 3)), 6: ((2, 1), (2, 3)),
-            8: ((3, 1), (3, 3)), 9: ((1, 2),), 10: ((2, 2),), 11: ((3, 2),)}
-FIRST_AT = {8: 0, 11: 1, 12: 2, 14: 3}
-SECOND_AT = {10: 0, 13: 1, 14: 2}
+            8: ((3, 1), (3, 3), (1, 2)), 9: ((2, 2),), 11: ((3, 2),)}
+FIRST_AT = {8: 0, 10: 1, 11: 2, 14: 3}
+SECOND_AT = {12: 1, 13: 2}
 SLOT = {place: k for k, place in enumerate(ORDER)}
 N_SLOT = len(ORDER)
 N_SEND = 67
@@ -260,18 +260,6 @@
 
     send_second(3)
 
-    stores = []
-    for e in range(n_loc):
-        cols = pl.ds(e * width, width)
-        stores.append(pltpu.make_async_copy(acc_gu.at[:, cols], dwg_ref.at[e], load_sem.at[len(stores)]))
-        stores.append(pltpu.make_async_copy(acc_gu.at[:, pl.ds(loc + e * width, width)], dwu_ref.at[e], load_sem.at[len(stores)]))
-        stores.append(pltpu.make_async_copy(acc_d.at[cols], dwd_ref.at[e], load_sem.at[len(stores)]))
-    for c in stores:
-        c.start()
-    dbias_ref[...] = acc_d[loc:loc + 1]
-    for j in range(N_SLOT - LAG, N_SLOT):
-        add_sibling(j)
-
     k2, k1, k3 = SLOT[(2, 0)], SLOT[(1, 0)], SLOT[(3, 0)]
 
     def wait_second(df):
@@ -299,6 +287,18 @@
         if df == 2:
             for c in f_first:
                 c.start()
+            send_second(0)
+            stores = []
+            for e in range(n_loc):
+                cols = pl.ds(e * width, width)
+                stores.append(pltpu.make_async_copy(acc_gu.at[:, cols], dwg_ref.at[e], load_sem.at[len(stores)]))
+                stores.append(pltpu.make_async_copy(acc_gu.at[:, pl.ds(loc + e * width, width)], dwu_ref.at[e], load_sem.at[len(stores)]))
+                stores.append(pltpu.make_async_copy(acc_d.at[cols], dwd_ref.at[e], load_sem.at[len(stores)]))
+            for c in stores:
+                c.start()
+            dbias_ref[...] = acc_d[loc:loc + 1]
+            for j in range(N_SLOT - LAG, N_SLOT):
+                add_sibling(j)
         if df == 1:
             f_first[0].wait_recv()
             pg_own[k1] = pg_own[k1] + r3g[...]

time: 127 us -> 128 us (level)
  no operation moved by 1% of the time
where the time goes in v6:
time: 128 us
  Pallas kernels  127 us (99%)
    pallas_call x1, Pallas kernels, moe(): pl.pallas_call(moe_kernel, name='moe', out_shape=out_shape, in_specs=[vme...  122 us
    pallas_call x1, Pallas kernels, finish(): pl.pallas_call(write_out, name='finish', out_shape=tuple((jax.ShapeDtypeS...  5.69 us

profile of v6, /device:TPU:97, one launch (start us, length us, event | category | flops | bytes accessed | tf_op | source)
XLA Modules:
  0.0 127.9 jit_solution(15109306678443176771)
XLA Ops:
  0.6 121.5 %moe.1 = (bf16[128,1024]{1,0:T(8,128)(2,1)}, bf16[128,1024]{1,0:T(8,128)(2,1)}, f32[1,1024]{1,0:T(1,128)}, f32[32,1024]{1,0:T(8,128)}, f32[1,1024]{1,0:T(1,128)}...) custom-call(bf16[128,1024]{1,0:T(8,128)(2,1)} %x_ref.1, bf16[128,1024]{1,0:T(8,128)(2,1)} %dy_ref.1, ...), custom_call_target="tpu_custom_call" | custom-call | tf_op jit(solution)/shard_map/moe/pallas_call | solution.py:436
  122.2 5.7 %finish.1 = (bf16[128,1024]{1,0:T(8,128)(2,1)}, bf16[128,1024]{1,0:T(8,128)(2,1)}, f32[1,1024]{1,0:T(1,128)}, f32[32,1024]{1,0:T(8,128)}, f32[4,1024,128]{2,1,0:...) custom-call(bf16[128,1024]{1,0:T(8,128)(2,1)} %get-tuple-element.24.refs_0_, ...), custom_call_target="tpu_custom_call" | custom-call | tf_op jit(solution)/shard_map/finish/pallas_call | solution.py:466

commit v7 on v5

--- a/solution.py
+++ b/solution.py
@@ -147,7 +147,7 @@
     def add_sibling(k):
         for c in to_sibling(k):
             c.wait_recv()
-        part[k] = (part[k].astype(F32) + q_buf[k].astype(F32)).astype(BF16)
+        part[k] = part[k] + q_buf[k]
         pg_own[k] = pg_own[k] + qg_buf[k]
 
     def s_first(df):
@@ -163,7 +163,7 @@
                 remote(part.at[k], r2.at[df, i], s2_send.at[df, i, 0], s2_recv.at[df, i, 0], dev))
 
     def add_into(k, t, block):
-        part[k, t] = (part[k, t].astype(F32) + block[...].astype(F32)).astype(BF16)
+        part[k, t] = part[k, t] + block[...]
 
     def send_second(df):
         for c in s_first(df):

time: 127 us -> 127 us (level)
  no operation moved by 1% of the time
where the time goes in v7:
time: 127 us
  Pallas kernels  126 us (99%)
    pallas_call x1, Pallas kernels, moe(): pl.pallas_call(moe_kernel, name='moe', out_shape=out_shape, in_specs=[vme...  120 us
    pallas_call x1, Pallas kernels, finish(): pl.pallas_call(write_out, name='finish', out_shape=tuple((jax.ShapeDtypeS...  5.69 us

profile of v7, /device:TPU:97, one launch (start us, length us, event | category | flops | bytes accessed | tf_op | source)
XLA Modules:
  0.0 126.6 jit_solution(13939104231692384589)
XLA Ops:
  0.6 120.3 %moe.1 = (bf16[128,1024]{1,0:T(8,128)(2,1)}, bf16[128,1024]{1,0:T(8,128)(2,1)}, f32[1,1024]{1,0:T(1,128)}, f32[32,1024]{1,0:T(8,128)}, f32[1,1024]{1,0:T(1,128)}...) custom-call(bf16[128,1024]{1,0:T(8,128)(2,1)} %x_ref.1, bf16[128,1024]{1,0:T(8,128)(2,1)} %dy_ref.1, ...), custom_call_target="tpu_custom_call" | custom-call | tf_op jit(solution)/shard_map/moe/pallas_call | solution.py:436
  120.9 5.7 %finish.1 = (bf16[128,1024]{1,0:T(8,128)(2,1)}, bf16[128,1024]{1,0:T(8,128)(2,1)}, f32[1,1024]{1,0:T(1,128)}, f32[32,1024]{1,0:T(8,128)}, f32[4,1024,128]{2,1,0:...) custom-call(bf16[128,1024]{1,0:T(8,128)(2,1)} %get-tuple-element.24.refs_0_, ...), custom_call_target="tpu_custom_call" | custom-call | tf_op jit(solution)/shard_map/finish/pallas_call | solution.py:466
